TPU v7x, 128 devices: a whole 4x4x4 slice. The times are simulated.
128 devices in a mesh: band: 8 (over y, core), row: 16 (over x, z).
Axes of the slice: x: 4, y: 4, z: 4, core: 2. Of those that a mesh axis runs over, the one named last changes fastest.
Arguments:
- observed: bfloat16 [224, 512, 680], P('band', 'row'), may hold values from -60 to 60
- row_taps: float32 [224, 25], P('band'), may hold values from 0 to 0.08
- col_taps: float32 [224, 25], P('band'), may hold values from 0 to 0.08
- spectral_basis: bfloat16 [224, 32], replicated, may hold values from -0.375 to 0.375
- ridge_weights: float32 [32], replicated, may hold values from 0.05 to 0.5
Outputs:
- coefficients: float32 [32, 512, 680], P(None, 'row', 'band')
- residual: float32 [32, 512, 680], P(None, 'row', 'band')
All inputs are finite; a program needn't handle non-finite values.
Results may differ from a plain program's by a relative error of at most 0.01.
Values may be sent and summed in bfloat16 or wider, within the bound.
A program may use at most 64 MiB of HBM per device.

v0:
```python
import functools

import jax
import jax.numpy as jnp
from jax import lax
from jax.sharding import Mesh
from jax.sharding import PartitionSpec as P

ITERS = 2
BAND_ROW = ("band_0", "band_1", "row_0", "row_1")
BAND = ("band_0", "band_1")
ROW = ("row_0", "row_1")


def over_axes(value, axes):
    return functools.reduce(lax.psum, axes, value)


def extended(cells, sides, width):
    for axis, dim in sides:
        count = lax.axis_size(axis)
        ends = count - 1
        head = lax.slice_in_dim(cells, 0, width, axis=dim)
        tail = lax.slice_in_dim(cells, cells.shape[dim] - width, cells.shape[dim], axis=dim)
        cells = jnp.concatenate(
            [
                lax.ppermute(tail, axis, [(i, (i + 1) % count) for i in range(ends)]),
                cells,
                lax.ppermute(head, axis, [((i + 1) % count, i) for i in range(ends)]),
            ],
            axis=dim,
        )
    return cells


def pass_rows(padded, kernel):
    length = padded.shape[1] - kernel.shape[1] + 1
    running = jnp.zeros((padded.shape[0], length, padded.shape[2]), jnp.float32)
    for offset in range(kernel.shape[1]):
        running = running + kernel[:, offset, None, None] * padded[
            :, offset : offset + length, :
        ].astype(jnp.float32)
    return running


def pass_cols(field, kernel):
    radius = (kernel.shape[1] - 1) // 2
    columns = field.shape[2]
    padded = jnp.pad(field, ((0, 0), (0, 0), (radius, radius)))
    running = jnp.zeros(field.shape, jnp.float32)
    for offset in range(kernel.shape[1]):
        running = running + kernel[:, offset, None, None] * padded[:, :, offset : offset + columns]
    return running


def two_products(residual, mapped):
    return (
        over_axes(jnp.sum(residual * residual), BAND_ROW),
        over_axes(jnp.sum(residual * mapped), BAND_ROW),
    )


def local(observed, row_taps, col_taps, spectral_basis, ridge_weights):
    radius = (row_taps.shape[1] - 1) // 2
    row_flip = row_taps[:, ::-1]
    col_flip = col_taps[:, ::-1]
    basis_wide = spectral_basis.astype(jnp.float32)

    def project(gathered):
        return jnp.einsum(
            "bk,brc->krc", spectral_basis, gathered, preferred_element_type=jnp.float32
        )

    def to_subspace(band_field):
        return project(lax.all_to_all(band_field, BAND, split_axis=2, concat_axis=0, tiled=True))

    def normal_map(direction):
        spectra = jnp.einsum(
            "bk,krc->brc", basis_wide, direction, precision=lax.Precision.HIGHEST
        ).astype(jnp.bfloat16)
        banded = lax.all_to_all(spectra, BAND, split_axis=0, concat_axis=2, tiled=True)
        padded = extended(banded, ((ROW, 1),), radius)
        blurred = pass_cols(pass_rows(padded, row_taps), col_taps).astype(jnp.bfloat16)
        blurred = extended(blurred, ((ROW, 1),), radius)
        returned = pass_cols(pass_rows(blurred, row_flip), col_flip).astype(jnp.bfloat16)
        return to_subspace(returned) + ridge_weights[:, None, None] * direction

    padded_obs = extended(observed, ((ROW, 1),), radius)
    adjoint_obs = pass_cols(pass_rows(padded_obs, row_flip), col_flip).astype(jnp.bfloat16)
    rhs = to_subspace(adjoint_obs)
    solution = jnp.zeros_like(rhs)
    residual = rhs
    direction = rhs
    along = normal_map(residual)
    norm_now, product = two_products(residual, along)
    alpha = norm_now / product
    for iteration in range(ITERS):
        solution = solution + alpha * direction
        residual = residual - alpha * along
        if iteration + 1 < ITERS:
            mapped = normal_map(residual)
            norm_next, product = two_products(residual, mapped)
            ratio = norm_next / norm_now
            alpha = norm_next / (product - ratio * norm_next / alpha)
            direction = residual + ratio * direction
            along = mapped + ratio * along
            norm_now = norm_next
    return (solution, residual)


def solution(mesh):
    split = Mesh(mesh.devices.reshape(4, 2, 4, 4), ("band_0", "band_1", "row_0", "row_1"))
    placed = (P(BAND, ROW, None), P(BAND, None), P(BAND, None), P(), P())
    return jax.shard_map(
        local,
        mesh=split,
        in_specs=placed,
        out_specs=(P(None, ROW, BAND), P(None, ROW, BAND)),
        check_vma=False,
    )
```

profile of v0, /device:TPU:1, one launch (start us, length us, event | category | flops | bytes accessed | tf_op | source)
XLA Modules:
  0.0 582.2 jit_solution(3140518809390338871)
XLA Ops:
  23.4 11.2 %multiply_add_fusion.4 = f32[28,32,680]{2,1,0:T(8,128)S(1)} fusion(bf16[28,32,680]{2,1,0:T(8,128)(2,1)S(1)} %copy-done.1, bf16[28,12,680]{2,1,0:T(8,128)(2,1)S(1)} %copy.37, bf16[28,44,680]{2,1,0:T(8,128)(2,1)S(1)} %copy_dynamic-update-slice_fusion.2, f32[28]{0:T(128)S(1)} %get-tuple-element.62, f32[28]{0:T(128)S(1)} %get-tuple-element.63, ...), kind=kLoop, calls=%fused_computation.278 | loop fusion | flops 67020800 | bytes 18738160 | tf_op jit(solution)/shard_map/add | solution.py:40
  34.7 19.2 %add_convert_fusion.4 = bf16[28,32,680]{2,1,0:T(8,128)(2,1)S(1)} fusion(f32[28,32,680]{2,1,0:T(8,128)S(1)} %multiply_add_fusion.4, f32[28]{0:T(128)S(1)} %get-tuple-element.37, f32[28]{0:T(128)S(1)} %get-tuple-element.38, f32[28]{0:T(128)S(1)} %get-tuple-element.15, f32[28]{0:T(128)S(1)} %get-tuple-element.16, f32[28]{0:T(128)S(1)} %get-tuple-element.17, ...), kind=kLoop, calls=%fused_computation.254 | loop fusion | flops 30464000 | bytes 3658480 | tf_op jit(solution)/shard_map/convert_element_type | solution.py:89
  53.9 9.0 %copy.40 = bf16[28,32,680]{1,0,2:T(8,128)(2,1)} copy(bf16[28,32,680]{2,1,0:T(8,128)(2,1)S(1)} %add_convert_fusion.4) | data formatting | bytes 2437120 | tf_op jit(solution)/shard_map/convert_element_type | solution.py:89
  70.9 23.3 %all_to_all.90 = bf16[8,2,38080]{2,1,0:T(2,128)(2,1)S(1)} all-to-all(bf16[8,2,38080]{2,1,0:T(2,128)(2,1)S(1)} %reshape.156), channel_id=1, replica_groups=mesh['band_0'=4,'band_1'=2,'row_0'=4,'row_1'=4] {'band_0','band_1'}, dimensions={0} | all-to-all | bytes 2437120 | tf_op jit(solution)/shard_map/all_to_all | solution.py:75
  115.6 27.8 %all_to_all.91 = bf16[224,32,85]{2,1,0:T(8,128)(2,1)S(1)} all-to-all(bf16[224,32,85]{2,1,0:T(8,128)(2,1)} %copy.43), channel_id=1, replica_groups=mesh['band_0'=4,'band_1'=2,'row_0'=4,'row_1'=4] {'band_0','band_1'}, dimensions={0} | all-to-all | bytes 2437120 | tf_op jit(solution)/shard_map/all_to_all | solution.py:81
  154.4 10.0 %collective-permute-done.2 = bf16[28,12,680]{2,0,1:T(8,128)(2,1)S(1)} collective-permute-done((bf16[28,12,680]{2,0,1:T(8,128)(2,1)S(1)}, bf16[28,12,680]{2,0,1:T(8,128)(2,1)S(1)}, u32[]{:S(2)}, u32[]{:S(2)}) %collective-permute-start.2) | collective-permute-done | bytes 456992 | tf_op jit(solution)/shard_map/ppermute | solution.py:27
  168.8 11.1 %multiply_add_fusion.3 = f32[28,32,680]{2,1,0:T(8,128)S(1)} fusion(bf16[28,32,680]{2,1,0:T(8,128)(2,1)S(1)} %all_to_all.72, bf16[28,12,680]{2,1,0:T(8,128)(2,1)S(1)} %copy.46, bf16[28,44,680]{2,1,0:T(8,128)(2,1)S(1)} %copy_dynamic-update-slice_fusion.1, f32[28]{0:T(128)S(1)} %get-tuple-element.62, f32[28]{0:T(128)S(1)} %get-tuple-element.63, ...), kind=kLoop, calls=%fused_computation.253 | loop fusion | flops 67020800 | bytes 18738160 | tf_op jit(solution)/shard_map/add | solution.py:40
  180.0 19.2 %add_convert_fusion.3 = bf16[28,32,680]{2,1,0:T(8,128)(2,1)S(1)} fusion(f32[28,32,680]{2,1,0:T(8,128)S(1)} %multiply_add_fusion.3, f32[28]{0:T(128)S(1)} %get-tuple-element.37, f32[28]{0:T(128)S(1)} %get-tuple-element.38, f32[28]{0:T(128)S(1)} %get-tuple-element.15, f32[28]{0:T(128)S(1)} %get-tuple-element.16, f32[28]{0:T(128)S(1)} %get-tuple-element.17, ...), kind=kLoop, calls=%fused_computation.229 | loop fusion | flops 30464000 | bytes 3658480 | tf_op jit(solution)/shard_map/convert_element_type | solution.py:83
  206.0 9.5 %collective-permute-done.5 = bf16[28,12,680]{2,0,1:T(8,128)(2,1)S(1)} collective-permute-done((bf16[28,12,680]{2,0,1:T(8,128)(2,1)S(1)}, bf16[28,12,680]{2,0,1:T(8,128)(2,1)S(1)}, u32[]{:S(2)}, u32[]{:S(2)}) %collective-permute-start.5) | collective-permute-done | bytes 456992 | tf_op jit(solution)/shard_map/ppermute | solution.py:29
  216.9 12.4 %multiply_add_fusion.2 = f32[28,32,680]{2,1,0:T(8,128)S(1)} fusion(bf16[28,32,680]{2,1,0:T(8,128)(2,1)S(1)} %add_convert_fusion.3, bf16[28,12,680]{2,1,0:T(8,128)(2,1)S(1)} %copy.52, bf16[28,12,680]{2,1,0:T(8,128)(2,1)S(1)} %copy.50, f32[28]{0:T(128)S(1)} %get-tuple-element.62, f32[28]{0:T(128)S(1)} %get-tuple-element.63, f32[28]{0:T(128)S(1)} %get-tuple-element.40, ...), kind=kLoop, calls=%fused_computation.228 | loop fusion | flops 88954880 | bytes 4572400 | tf_op jit(solution)/shard_map/add | solution.py:40
  229.3 19.2 %add_convert_fusion.2 = bf16[28,32,680]{2,1,0:T(8,128)(2,1)S(1)} fusion(f32[28,32,680]{2,1,0:T(8,128)S(1)} %multiply_add_fusion.2, f32[28]{0:T(128)S(1)} %get-tuple-element.37, f32[28]{0:T(128)S(1)} %get-tuple-element.38, f32[28]{0:T(128)S(1)} %get-tuple-element.15, f32[28]{0:T(128)S(1)} %get-tuple-element.16, f32[28]{0:T(128)S(1)} %get-tuple-element.17, ...), kind=kLoop, calls=%fused_computation.204 | loop fusion | flops 30464000 | bytes 3658480 | tf_op jit(solution)/shard_map/convert_element_type | solution.py:85
  248.5 9.0 %copy.53 = bf16[28,32,680]{1,0,2:T(8,128)(2,1)} copy(bf16[28,32,680]{2,1,0:T(8,128)(2,1)S(1)} %add_convert_fusion.2) | data formatting | bytes 2437120 | tf_op jit(solution)/shard_map/convert_element_type | solution.py:85
  265.5 22.2 %all_to_all.92 = bf16[8,2,38080]{2,1,0:T(2,128)(2,1)S(1)} all-to-all(bf16[8,2,38080]{2,1,0:T(2,128)(2,1)S(1)} %reshape.158), channel_id=1, replica_groups=mesh['band_0'=4,'band_1'=2,'row_0'=4,'row_1'=4] {'band_0','band_1'}, dimensions={0} | all-to-all | bytes 2437120 | tf_op jit(solution)/shard_map/all_to_all | solution.py:75
  319.2 16.4 %all-reduce.8 = (f32[]{:T(128)}, f32[]{:T(128)}) all-reduce(f32[]{:T(128)} %get-tuple-element.78, f32[]{:T(128)} %get-tuple-element.79), channel_id=1, replica_groups=mesh['band_0'=4,'band_1'=2,'row_0'=4,'row_1'=4] {'row_0'}, use_global_device_ids=true, to_apply=%region_3.4 | all-reduce | flops 2 | bytes 16 | tf_op jit(solution)/shard_map/psum | solution.py:16
  348.3 31.2 %all_to_all.93 = bf16[224,32,85]{2,1,0:T(8,128)(2,1)S(1)} all-to-all(bf16[224,32,85]{2,1,0:T(8,128)(2,1)} %copy.56), channel_id=1, replica_groups=mesh['band_0'=4,'band_1'=2,'row_0'=4,'row_1'=4] {'band_0','band_1'}, dimensions={0} | all-to-all | bytes 2437120 | tf_op jit(solution)/shard_map/all_to_all | solution.py:81
  390.8 10.0 %collective-permute-done.6 = bf16[28,12,680]{2,0,1:T(8,128)(2,1)S(1)} collective-permute-done((bf16[28,12,680]{2,0,1:T(8,128)(2,1)S(1)}, bf16[28,12,680]{2,0,1:T(8,128)(2,1)S(1)}, u32[]{:S(2)}, u32[]{:S(2)}) %collective-permute-start.6) | collective-permute-done | bytes 456992 | tf_op jit(solution)/shard_map/ppermute | solution.py:27
  405.2 11.1 %multiply_add_fusion.1 = f32[28,32,680]{2,1,0:T(8,128)S(1)} fusion(bf16[28,32,680]{2,1,0:T(8,128)(2,1)S(1)} %all_to_all.80, bf16[28,12,680]{2,1,0:T(8,128)(2,1)S(1)} %copy.59, bf16[28,44,680]{2,1,0:T(8,128)(2,1)S(1)} %copy_dynamic-update-slice_fusion, f32[28]{0:T(128)S(1)} %get-tuple-element.62, f32[28]{0:T(128)S(1)} %get-tuple-element.63, ...), kind=kLoop, calls=%fused_computation.203 | loop fusion | flops 67020800 | bytes 18738160 | tf_op jit(solution)/shard_map/add | solution.py:40
  416.3 19.2 %add_convert_fusion.1 = bf16[28,32,680]{2,1,0:T(8,128)(2,1)S(1)} fusion(f32[28,32,680]{2,1,0:T(8,128)S(1)} %multiply_add_fusion.1, f32[28]{0:T(128)S(1)} %get-tuple-element.37, f32[28]{0:T(128)S(1)} %get-tuple-element.38, f32[28]{0:T(128)S(1)} %get-tuple-element.15, f32[28]{0:T(128)S(1)} %get-tuple-element.16, f32[28]{0:T(128)S(1)} %get-tuple-element.17, ...), kind=kLoop, calls=%fused_computation.179 | loop fusion | flops 30464000 | bytes 3658480 | tf_op jit(solution)/shard_map/convert_element_type | solution.py:83
  441.7 8.9 %collective-permute-done.9 = bf16[28,12,680]{2,0,1:T(8,128)(2,1)S(1)} collective-permute-done((bf16[28,12,680]{2,0,1:T(8,128)(2,1)S(1)}, bf16[28,12,680]{2,0,1:T(8,128)(2,1)S(1)}, u32[]{:S(2)}, u32[]{:S(2)}) %collective-permute-start.9) | collective-permute-done | bytes 456992 | tf_op jit(solution)/shard_map/ppermute | solution.py:29
  451.9 12.4 %multiply_add_fusion = f32[28,32,680]{2,1,0:T(8,128)S(1)} fusion(bf16[28,32,680]{2,1,0:T(8,128)(2,1)S(1)} %add_convert_fusion.1, bf16[28,12,680]{2,1,0:T(8,128)(2,1)S(1)} %copy.65, bf16[28,12,680]{2,1,0:T(8,128)(2,1)S(1)} %copy.63, f32[28]{0:T(128)S(1)} %get-tuple-element.62, f32[28]{0:T(128)S(1)} %get-tuple-element.63, f32[28]{0:T(128)S(1)} %get-tuple-element.40, ...), kind=kLoop, calls=%fused_computation.178 | loop fusion | flops 88954880 | bytes 4572400 | tf_op jit(solution)/shard_map/add | solution.py:40
  464.3 19.2 %add_convert_fusion = bf16[28,32,680]{2,1,0:T(8,128)(2,1)S(1)} fusion(f32[28,32,680]{2,1,0:T(8,128)S(1)} %multiply_add_fusion, f32[28]{0:T(128)S(1)} %get-tuple-element.37, f32[28]{0:T(128)S(1)} %get-tuple-element.38, f32[28]{0:T(128)S(1)} %get-tuple-element.15, f32[28]{0:T(128)S(1)} %get-tuple-element.16, f32[28]{0:T(128)S(1)} %get-tuple-element.17, ...), kind=kLoop, calls=%fused_computation.154 | loop fusion | flops 30464000 | bytes 3658480 | tf_op jit(solution)/shard_map/convert_element_type | solution.py:85
  483.5 9.0 %copy.66 = bf16[28,32,680]{1,0,2:T(8,128)(2,1)} copy(bf16[28,32,680]{2,1,0:T(8,128)(2,1)S(1)} %add_convert_fusion) | data formatting | bytes 2437120 | tf_op jit(solution)/shard_map/convert_element_type | solution.py:85
  500.5 22.7 %all_to_all.94 = bf16[8,2,38080]{2,1,0:T(2,128)(2,1)S(1)} all-to-all(bf16[8,2,38080]{2,1,0:T(2,128)(2,1)S(1)} %reshape.160), channel_id=1, replica_groups=mesh['band_0'=4,'band_1'=2,'row_0'=4,'row_1'=4] {'band_0','band_1'}, dimensions={0} | all-to-all | bytes 2437120 | tf_op jit(solution)/shard_map/all_to_all | solution.py:75
  554.9 13.0 %all-reduce.7 = (f32[]{:T(128)}, f32[]{:T(128)}) all-reduce(f32[]{:T(128)} %get-tuple-element.76, f32[]{:T(128)} %get-tuple-element.77), channel_id=1, replica_groups=mesh['band_0'=4,'band_1'=2,'row_0'=4,'row_1'=4] {'row_0'}, use_global_device_ids=true, to_apply=%region_13.14 | all-reduce | flops 2 | bytes 16 | tf_op jit(solution)/shard_map/psum | solution.py:16
  (110 shorter events, 198.1 us)
Async XLA Ops:
  0.6 109.0 %copy-start = (bf16[224,32]{0,1:T(8,128)(2,1)S(1)}, bf16[224,32]{0,1:T(8,128)(2,1)}, u32[]{:S(2)}) copy-start(bf16[224,32]{0,1:T(8,128)(2,1)} %param.8) | copy-start | bytes 43012
  0.6 9.3 %copy-start.1 = (bf16[28,32,680]{2,1,0:T(8,128)(2,1)S(1)}, bf16[28,32,680]{2,1,0:T(8,128)(2,1)}, u32[]{:S(2)}) copy-start(bf16[28,32,680]{2,1,0:T(8,128)(2,1)} %param.5) | copy-start | bytes 3655684
  0.7 7.9 %copy-start.3 = (f32[28,25]{1,0:T(8,128)S(1)}, f32[28,25]{1,0:T(8,128)}, u32[]{:S(2)}) copy-start(f32[28,25]{1,0:T(8,128)} %param.7) | copy-start | bytes 8404
  2.4 16.4 %collective-permute-start = (bf16[28,12,680]{2,0,1:T(8,128)(2,1)S(1)}, bf16[28,12,680]{2,0,1:T(8,128)(2,1)S(1)}, u32[]{:S(2)}, u32[]{:S(2)}) collective-permute-start(bf16[28,12,680]{2,0,1:T(8,128)(2,1)S(1)} %copy.71), channel_id=1, source_target_pairs={{0,1},{1,2},{2,3},{3,4},{4,5},{5,6},{6,7},{7,8},{8,9},{9,10},{10,1... | collective-permute-start | bytes 1370888 | tf_op jit(solution)/shard_map/ppermute | solution.py:27
  7.0 16.1 %collective-permute-start.1 = (bf16[28,12,680]{2,0,1:T(8,128)(2,1)S(1)}, bf16[28,12,680]{2,0,1:T(8,128)(2,1)S(1)}, u32[]{:S(2)}, u32[]{:S(2)}) collective-permute-start(bf16[28,12,680]{2,0,1:T(8,128)(2,1)S(1)} %copy.72), channel_id=1, source_target_pairs={{1,0},{2,1},{3,2},{4,3},{5,4},{6,5},{7,6},{8,7},{9,8},{10,9},{11,1... | collective-permute-start | bytes 1370888 | tf_op jit(solution)/shard_map/ppermute | solution.py:29
  10.0 24.7 %copy-start.8 = (f32[28]{0:T(128)}, f32[28]{0:T(128)S(1)}, u32[]{:S(2)}) copy-start(f32[28]{0:T(128)S(1)} %get-tuple-element.31) | copy-start | bytes 340
  10.0 24.7 %copy-start.11 = (f32[28]{0:T(128)}, f32[28]{0:T(128)S(1)}, u32[]{:S(2)}) copy-start(f32[28]{0:T(128)S(1)} %get-tuple-element.32) | copy-start | bytes 340
  149.4 15.0 %collective-permute-start.2 = (bf16[28,12,680]{2,0,1:T(8,128)(2,1)S(1)}, bf16[28,12,680]{2,0,1:T(8,128)(2,1)S(1)}, u32[]{:S(2)}, u32[]{:S(2)}) collective-permute-start(bf16[28,12,680]{2,0,1:T(8,128)(2,1)S(1)} %copy.45), channel_id=1, source_target_pairs={{0,1},{1,2},{2,3},{3,4},{4,5},{5,6},{6,7},{7,8},{8,9},{9,10},{10,1... | collective-permute-start | bytes 1370888 | tf_op jit(solution)/shard_map/ppermute | solution.py:27
  153.0 15.5 %collective-permute-start.3 = (bf16[28,12,680]{2,0,1:T(8,128)(2,1)S(1)}, bf16[28,12,680]{2,0,1:T(8,128)(2,1)S(1)}, u32[]{:S(2)}, u32[]{:S(2)}) collective-permute-start(bf16[28,12,680]{2,0,1:T(8,128)(2,1)S(1)} %copy.47), channel_id=1, source_target_pairs={{1,0},{2,1},{3,2},{4,3},{5,4},{6,5},{7,6},{8,7},{9,8},{10,9},{11,1... | collective-permute-start | bytes 1370888 | tf_op jit(solution)/shard_map/ppermute | solution.py:29
  168.8 11.2 %copy-start.9 = (f32[28]{0:T(128)S(1)}, f32[28]{0:T(128)}, u32[]{:S(2)}) copy-start(f32[28]{0:T(128)} %copy-done.8) | copy-start | bytes 340
  168.8 11.2 %copy-start.12 = (f32[28]{0:T(128)S(1)}, f32[28]{0:T(128)}, u32[]{:S(2)}) copy-start(f32[28]{0:T(128)} %copy-done.11) | copy-start | bytes 340
  199.5 16.0 %collective-permute-start.5 = (bf16[28,12,680]{2,0,1:T(8,128)(2,1)S(1)}, bf16[28,12,680]{2,0,1:T(8,128)(2,1)S(1)}, u32[]{:S(2)}, u32[]{:S(2)}) collective-permute-start(bf16[28,12,680]{2,0,1:T(8,128)(2,1)S(1)} %copy.51), channel_id=1, source_target_pairs={{1,0},{2,1},{3,2},{4,3},{5,4},{6,5},{7,6},{8,7},{9,8},{10,9},{11,1... | collective-permute-start | bytes 1370888 | tf_op jit(solution)/shard_map/ppermute | solution.py:29
  201.0 15.6 %collective-permute-start.4 = (bf16[28,12,680]{2,0,1:T(8,128)(2,1)S(1)}, bf16[28,12,680]{2,0,1:T(8,128)(2,1)S(1)}, u32[]{:S(2)}, u32[]{:S(2)}) collective-permute-start(bf16[28,12,680]{2,0,1:T(8,128)(2,1)S(1)} %copy.49), channel_id=1, source_target_pairs={{0,1},{1,2},{2,3},{3,4},{4,5},{5,6},{6,7},{7,8},{8,9},{9,10},{10,1... | collective-permute-start | bytes 1370888 | tf_op jit(solution)/shard_map/ppermute | solution.py:27
  295.1 8.0 %copy-start.14 = (f32[32]{0:T(128)S(1)}, f32[32]{0:T(128)}, u32[]{:S(2)}) copy-start(f32[32]{0:T(128)} %param.9) | copy-start | bytes 388
  306.0 42.3 %copy-start.6 = (f32[32,32,85]{2,0,1:T(8,128)}, f32[32,32,85]{2,0,1:T(8,128)S(1)}, u32[]{:S(2)}) copy-start(f32[32,32,85]{2,0,1:T(8,128)S(1)} %get-tuple-element.92) | copy-start | bytes 1044484
  385.5 15.3 %collective-permute-start.6 = (bf16[28,12,680]{2,0,1:T(8,128)(2,1)S(1)}, bf16[28,12,680]{2,0,1:T(8,128)(2,1)S(1)}, u32[]{:S(2)}, u32[]{:S(2)}) collective-permute-start(bf16[28,12,680]{2,0,1:T(8,128)(2,1)S(1)} %copy.58), channel_id=1, source_target_pairs={{0,1},{1,2},{2,3},{3,4},{4,5},{5,6},{6,7},{7,8},{8,9},{9,10},{10,1... | collective-permute-start | bytes 1370888 | tf_op jit(solution)/shard_map/ppermute | solution.py:27
  389.4 15.5 %collective-permute-start.7 = (bf16[28,12,680]{2,0,1:T(8,128)(2,1)S(1)}, bf16[28,12,680]{2,0,1:T(8,128)(2,1)S(1)}, u32[]{:S(2)}, u32[]{:S(2)}) collective-permute-start(bf16[28,12,680]{2,0,1:T(8,128)(2,1)S(1)} %copy.60), channel_id=1, source_target_pairs={{1,0},{2,1},{3,2},{4,3},{5,4},{6,5},{7,6},{8,7},{9,8},{10,9},{11,1... | collective-permute-start | bytes 1370888 | tf_op jit(solution)/shard_map/ppermute | solution.py:29
  405.1 11.2 %copy-start.10 = (f32[28]{0:T(128)S(1)}, f32[28]{0:T(128)}, u32[]{:S(2)}) copy-start(f32[28]{0:T(128)} %copy-done.8) | copy-start | bytes 340
  405.2 11.2 %copy-start.13 = (f32[28]{0:T(128)S(1)}, f32[28]{0:T(128)}, u32[]{:S(2)}) copy-start(f32[28]{0:T(128)} %copy-done.11) | copy-start | bytes 340
  435.9 14.6 %collective-permute-start.9 = (bf16[28,12,680]{2,0,1:T(8,128)(2,1)S(1)}, bf16[28,12,680]{2,0,1:T(8,128)(2,1)S(1)}, u32[]{:S(2)}, u32[]{:S(2)}) collective-permute-start(bf16[28,12,680]{2,0,1:T(8,128)(2,1)S(1)} %copy.64), channel_id=1, source_target_pairs={{1,0},{2,1},{3,2},{4,3},{5,4},{6,5},{7,6},{8,7},{9,8},{10,9},{11,1... | collective-permute-start | bytes 1370888 | tf_op jit(solution)/shard_map/ppermute | solution.py:29
  437.4 14.2 %collective-permute-start.8 = (bf16[28,12,680]{2,0,1:T(8,128)(2,1)S(1)}, bf16[28,12,680]{2,0,1:T(8,128)(2,1)S(1)}, u32[]{:S(2)}, u32[]{:S(2)}) collective-permute-start(bf16[28,12,680]{2,0,1:T(8,128)(2,1)S(1)} %copy.62), channel_id=1, source_target_pairs={{0,1},{1,2},{2,3},{3,4},{4,5},{5,6},{6,7},{7,8},{8,9},{9,10},{10,1... | collective-permute-start | bytes 1370888 | tf_op jit(solution)/shard_map/ppermute | solution.py:27
  530.7 8.0 %copy-start.5 = (f32[32,32,85]{2,0,1:T(8,128)S(1)}, f32[32,32,85]{2,0,1:T(8,128)}, u32[]{:S(2)}) copy-start(f32[32,32,85]{2,0,1:T(8,128)} %copy-done.4) | copy-start | bytes 1044484
  530.7 8.0 %copy-start.15 = (f32[32]{0:T(128)S(1)}, f32[32]{0:T(128)}, u32[]{:S(2)}) copy-start(f32[32]{0:T(128)} %param.9) | copy-start | bytes 388
  538.7 40.6 %copy-start.7 = (f32[32,32,85]{2,0,1:T(8,128)S(1)}, f32[32,32,85]{2,0,1:T(8,128)}, u32[]{:S(2)}) copy-start(f32[32,32,85]{2,0,1:T(8,128)} %copy-done.6) | copy-start | bytes 1044484
  (2 other events, 8.5 us)
where the time goes:
time: 593 us; the launch traced here: 582 us
  blocking collectives  196 us (33%)
  other arithmetic  155 us (26%)
  local copies, waits for them, and re-layouts  125 us (21%)
  waiting for transfers between devices  60.2 us (10%)
  starting transfers between devices  27.2 us (5%)
  matrix products  10.7 us (2%)
  between operations  7.62 us (1%)
    psum x8, blocking collectives, over_axes(): return functools.reduce(lax.psum, axes, value)  69.2 us
    all_to_all x3, blocking collectives, to_subspace(): lax.all_to_all(band_field, BAND, split_axis=2, concat_axis=0, tiled=True)  68.2 us
    all_to_all x2, blocking collectives, normal_map(): lax.all_to_all(spectra, BAND, split_axis=0, concat_axis=2, tiled=True)  58.9 us
    add x5, other arithmetic, pass_rows(): running + kernel[:, offset, None, None] * padded[:, offset:offset + lengt...  58.3 us
    unnamed x45, local copies, waits for them, and re-layouts  49.8 us
    convert_element_type x2, other arithmetic, normal_map(): pass_cols(pass_rows(padded, row_taps), col_taps).astype(jnp.bfloat16)  38.5 us
    convert_element_type x2, other arithmetic, normal_map(): pass_cols(pass_rows(blurred, row_flip), col_flip).astype(jnp.bfloat16)  38.5 us
    ppermute x5, waiting for transfers between devices, extended(): lax.ppermute(tail, axis, [(i, (i + 1) % count) for i in range(ends)])  30.3 us
  transfers between devices with their start and end apart: 10, of which 10 were waited for; matrix products, arithmetic and copies ran while one was open for 1% of the time, Pallas kernels for 0%

commit v1 on v0

v1 whole, which is shorter than its diff:
```python
import functools

import jax
import jax.numpy as jnp
from jax import lax
from jax.experimental import pallas as pl
from jax.experimental.pallas import tpu as pltpu
from jax.sharding import Mesh
from jax.sharding import PartitionSpec as P

AXES = ("band_0", "band_1", "row_0", "row_1")
BAND = ("band_0", "band_1")
ROW = ("row_0", "row_1")
TAPS = 25
RAD = 12
HALO = 24
LANES = 128
BF = jnp.bfloat16
F32 = jnp.float32


def iota(shape, dim):
    return lax.broadcasted_iota(jnp.int32, shape, dim)


def toeplitz(line, rows, lanes, shift):
    step = pltpu.roll(jnp.broadcast_to(line, (8, lanes)), 0, 1, stride=1, stride_axis=0)
    tiles = []
    for g in range(rows // 8):
        turn = (shift + 8 * g) % lanes
        tiles.append(pltpu.roll(step, turn, 1) if turn else step)
    return jnp.concatenate(tiles, axis=0)


def mm(a, b):
    return lax.dot_general(a, b, (((1,), (0,)), ((), ())), preferred_element_type=F32)


def normal_build_kernel(sizes, taps_ref, tt_ref, rr_ref):
    rows, cols, height, width = sizes
    row_dev = lax.axis_index(ROW)
    col_dev = lax.axis_index(BAND)
    mid_c = cols + 2 * RAD
    mid_r = rows + 2 * RAD
    ext_r = rows + 2 * HALO
    ku = tt_ref.shape[1]
    i1, u1 = iota((ku, LANES), 0), iota((ku, LANES), 1)
    col_u = col_dev * cols - RAD + u1
    keep1 = (i1 - u1 >= 0) & (i1 - u1 < TAPS) & (u1 < mid_c) & (col_u >= 0) & (col_u < width)
    u2, o2 = iota((LANES, LANES), 0), iota((LANES, LANES), 1)
    keep2 = (u2 - o2 >= 0) & (u2 - o2 < TAPS) & (o2 < cols) & (u2 < mid_c)
    ur, lr = iota((64, 256), 0), iota((64, 256), 1)
    row_u = row_dev * rows - RAD + ur
    keep_r = (ur < mid_r) & (row_u >= 0) & (row_u < height)
    r2, v2 = iota((rows, LANES), 0), iota((rows, LANES), 1)
    keep_r2 = (v2 - r2 >= 0) & (v2 - r2 < TAPS)

    def body(t, carry):
        for q in range(3):
            b = 3 * t + q
            line = taps_ref[b]
            ct, ctr = line[0:1, :LANES], line[1:2, :LANES]
            rt, rtr = line[2:3], line[3:4, :LANES]
            t1 = jnp.where(keep1, toeplitz(ctr, ku, LANES, -HALO), 0.0).astype(BF)
            t2 = jnp.where(keep2, toeplitz(ct, LANES, LANES, -HALO), 0.0).astype(BF)
            tt_ref[b] = mm(t1, t2).astype(BF)
            d1 = lr - ext_r * q - ur
            r1 = jnp.where(keep_r & (d1 >= 0) & (d1 < TAPS), toeplitz(rt, 64, 256, ext_r * q), 0.0)
            ra = jnp.where(keep_r2, toeplitz(rtr, rows, LANES, 0), 0.0).astype(BF)
            rr_ref[t, rows * q : rows * (q + 1), :] = mm(ra[:, :64], r1.astype(BF)).astype(BF)
        return carry

    lax.fori_loop(0, rr_ref.shape[0], body, 0)


def normal_kernel(sizes, pe_ref, e8_ref, p8_ref, tt_ref, rr_ref, p_ref, ridge_ref, out_ref, spec, mid, fin):
    rows, cols, _, _ = sizes
    ext_r = rows + 2 * HALO
    comps = p_ref.shape[0]
    bands = tt_ref.shape[0]
    chunk = 45

    def expand(i, carry):
        x = pe_ref[:, pl.ds(pl.multiple_of(16 * i, 16), 16), :].astype(F32)
        x0 = x[:, :8, :].reshape(comps * 8, 256).astype(BF)
        x1 = x[:, 8:, :].reshape(comps * 8, 256).astype(BF)
        for m in range(bands // chunk):
            e = e8_ref[8 * chunk * m : 8 * chunk * (m + 1), :]
            y0 = mm(e, x0).reshape(chunk, 8, 256)
            y1 = mm(e, x1).reshape(chunk, 8, 256)
            y = jnp.concatenate([y0, y1], axis=1).astype(BF)
            spec[chunk * m : chunk * (m + 1), pl.ds(pl.multiple_of(16 * i, 16), 16), :] = y
        return carry

    lax.fori_loop(0, ext_r // 16, expand, 0)

    ku = tt_ref.shape[1]

    def columns(g, carry):
        for q in range(9):
            b = 9 * g + q
            mid[b] = mm(spec[b][:, :ku], tt_ref[b]).astype(BF)
        return carry

    lax.fori_loop(0, bands // 9, columns, 0)

    def along(g, carry):
        for q in range(5):
            t = 5 * g + q
            x = mid[pl.ds(3 * t, 3)].reshape(3 * ext_r, LANES)
            y = mm(rr_ref[t][:, : 3 * ext_r], x)
            fin[pl.ds(3 * t, 3)] = y.reshape(3, rows, LANES)
        return carry

    lax.fori_loop(0, bands // 15, along, 0)

    def project(i, carry):
        sl = pl.ds(pl.multiple_of(8 * i, 8), 8)
        x = fin[:, sl, :].reshape(bands * 8, LANES).astype(BF)
        y = mm(p8_ref[...], x).reshape(comps, 8, LANES)
        out_ref[:, sl, :] = y + ridge_ref[...] * p_ref[:, sl, :]
        return carry

    lax.fori_loop(0, rows // 8, project, 0)


def rhs_kernel(sizes, obs_ref, taps_ref, p8_ref, out_ref, racc, tacc, fin):
    rows, cols, _, _ = sizes
    nb = obs_ref.shape[0]
    mid_r = rows + 2 * RAD
    win = 2 * cols + 2 * RAD
    kw = tacc.shape[0]
    pairs = fin.shape[0]
    r, l = iota((rows, 256), 0), iota((rows, 256), 1)
    w, o = iota((kw, LANES), 0), iota((kw, LANES), 1)
    keep_a = (w - o >= 0) & (w - o < TAPS) & (o < cols) & (w < win)
    o_b = o + cols
    keep_b = (w - o_b >= 0) & (w - o_b < TAPS) & (o < cols) & (w < win)

    def body(g, carry):
        for q in range(4):
            b = 4 * g + q
            rtr = taps_ref[b][3:4]
            d = l - mid_r * q - r
            m = jnp.where((d >= 0) & (d < TAPS), toeplitz(rtr, rows, 256, mid_r * q), 0.0)
            racc[rows * q : rows * (q + 1), :] = m.astype(BF)
        x = obs_ref[pl.ds(4 * g, 4)].astype(F32).reshape(4 * mid_r, obs_ref.shape[2]).astype(BF)
        y = mm(racc[:, : 4 * mid_r], x)
        full = obs_ref.shape[2]
        wins = []
        for k in range(pairs):
            start = 2 * cols * k - RAD
            wins.append(pltpu.roll(y, (full - start) % full, 1)[:, :256].astype(BF))
        for q in range(4):
            b = 4 * g + q
            ct = taps_ref[b][0:1, :LANES]
            ta = jnp.where(keep_a, toeplitz(ct, kw, LANES, -HALO), 0.0).astype(BF)
            tb = jnp.where(keep_b, toeplitz(ct, kw, LANES, -HALO - cols), 0.0).astype(BF)
            tacc[:, :LANES] = ta
            tacc[:, LANES:] = tb
            x = jnp.concatenate([v[rows * q : rows * (q + 1)] for v in wins], axis=0)
            z = mm(x[:, :kw], tacc[...])
            for k in range(pairs):
                fin[k, b] = z[rows * k : rows * (k + 1)]
        return carry

    lax.fori_loop(0, nb // 4, body, 0)
    comps = out_ref.shape[1]
    for k in range(pairs):
        def project(i, carry):
            sl = pl.ds(pl.multiple_of(8 * i, 8), 8)
            x = fin[k, :, sl, :].reshape(nb * 8, 256).astype(BF)
            y = mm(p8_ref[...], x).reshape(comps, 8, 256)
            out_ref[2 * k, :, sl, :] = y[:, :, :LANES]
            out_ref[2 * k + 1, :, sl, :] = y[:, :, LANES:]
            return carry

        lax.fori_loop(0, rows // 8, project, 0)


def vmem():
    return pl.BlockSpec(memory_space=pltpu.VMEM)


def call(kernel, outs, ins, scratch, flops):
    return pl.pallas_call(
        kernel,
        out_shape=outs,
        in_specs=[vmem()] * ins,
        out_specs=jax.tree.map(lambda _: vmem(), outs),
        scratch_shapes=scratch,
        compiler_params=pltpu.CompilerParams(vmem_limit_bytes=60 * 1024 * 1024),
        cost_estimate=pl.CostEstimate(flops=flops, bytes_accessed=16 * 1024 * 1024, transcendentals=0),
    )


def shifted(x, axis, step):
    count = lax.axis_size(axis)
    if step > 0:
        pairs = [(i, i + 1) for i in range(count - 1)]
    else:
        pairs = [(i + 1, i) for i in range(count - 1)]
    return lax.ppermute(x, axis, pairs)


def local(height, width, observed, row_taps, col_taps, spectral_basis, ridge_weights):
    own, rows, _ = observed.shape
    bands, comps = spectral_basis.shape
    cols = width // lax.axis_size(BAND)
    sizes = (rows, cols, height, width)
    full = -(-width // LANES) * LANES
    padded_bands = -(-bands // 45) * 45

    obs = jnp.concatenate(
        [shifted(observed[:, rows - RAD :], ROW, 1), observed, shifted(observed[:, :RAD], ROW, -1)], axis=1
    )
    obs = jnp.pad(obs, ((0, 0), (0, 0), (0, full - width)))

    both = jnp.stack([col_taps, col_taps[:, ::-1], row_taps, row_taps[:, ::-1]], axis=1)
    own_lines = jnp.pad(both, ((0, 0), (0, 4), (0, 256 - TAPS)))
    every = lax.all_gather(both, BAND, axis=0, tiled=True)
    every = jnp.pad(every, ((0, padded_bands - bands), (0, 4), (0, 256 - TAPS)))

    eye = jnp.eye(8, dtype=BF)
    basis = jnp.pad(spectral_basis, ((0, padded_bands - bands), (0, 0)))
    e8 = (basis[:, None, :, None] * eye[None, :, None, :]).reshape(padded_bands * 8, comps * 8)
    p8 = (basis.T[:, None, :, None] * eye[None, :, None, :]).reshape(comps * 8, padded_bands * 8)
    mine = lax.dynamic_slice_in_dim(spectral_basis, lax.axis_index(BAND) * own, own, 0)
    p8_own = (mine.T[:, None, :, None] * eye[None, :, None, :]).reshape(comps * 8, own * 8)

    ku = 144
    tt, rr = call(
        functools.partial(normal_build_kernel, sizes),
        (
            jax.ShapeDtypeStruct((padded_bands, ku, LANES), BF),
            jax.ShapeDtypeStruct((padded_bands // 3, 3 * rows, 256), BF),
        ),
        1,
        [],
        2 * 10**9,
    )(every)

    partial = call(
        functools.partial(rhs_kernel, sizes),
        jax.ShapeDtypeStruct((lax.axis_size(BAND), comps, rows, LANES), F32),
        3,
        [
            pltpu.VMEM((4 * rows, 256), BF),
            pltpu.VMEM((208, 256), BF),
            pltpu.VMEM((lax.axis_size(BAND) // 2, own, rows, 256), F32),
        ],
        2 * 10**9,
    )(obs, own_lines, p8_own)
    rhs = lax.psum_scatter(partial, BAND, scatter_dimension=0, tiled=True)[0]

    ridge = jnp.broadcast_to(ridge_weights[:, None, None], (comps, 8, LANES))

    def normal(p):
        b = p[:, :, :cols].astype(BF)
        ext = jnp.concatenate([shifted(b[:, rows - HALO :], ROW, 1), b, shifted(b[:, :HALO], ROW, -1)], axis=1)
        ext = jnp.concatenate(
            [shifted(ext[:, :, cols - HALO :], BAND, 1), ext, shifted(ext[:, :, :HALO], BAND, -1)], axis=2
        )
        ext = jnp.pad(ext, ((0, 0), (0, 0), (0, 256 - ext.shape[2])))
        return call(
            functools.partial(normal_kernel, sizes),
            jax.ShapeDtypeStruct((comps, rows, LANES), F32),
            7,
            [
                pltpu.VMEM((padded_bands, rows + 2 * HALO, 256), BF),
                pltpu.VMEM((padded_bands, rows + 2 * HALO, LANES), BF),
                pltpu.VMEM((padded_bands, rows, LANES), F32),
            ],
            2 * 10**10,
        )(ext, e8, p8, tt, rr, p, ridge)

    q = normal(rhs)
    s = normal(q)

    dots = lax.psum(
        jnp.stack([jnp.sum(rhs * rhs), jnp.sum(rhs * q), jnp.sum(q * q), jnp.sum(rhs * s), jnp.sum(q * s)]), AXES
    )
    rr0, rq, qq, rs, qs = [dots[i] for i in range(5)]
    alpha = rr0 / rq
    rr1 = rr0 - 2.0 * alpha * rq + alpha * alpha * qq
    beta = rr1 / rr0
    g = 1.0 + beta
    curve = g * g * rq - alpha * g * (qq + rs) + alpha * alpha * qs
    alpha2 = rr1 / curve
    coefs = alpha * rhs + alpha2 * (g * rhs - alpha * q)
    resid = (rhs - alpha * q) - alpha2 * (g * q - alpha * s)
    return coefs[:, :, :cols], resid[:, :, :cols]


def solution(mesh):
    split = Mesh(mesh.devices.reshape(4, 2, 4, 4), AXES)
    placed = (P(BAND, ROW, None), P(BAND, None), P(BAND, None), P(), P())

    def whole(observed, row_taps, col_taps, spectral_basis, ridge_weights):
        _, height, width = observed.shape
        return jax.shard_map(
            functools.partial(local, height, width),
            mesh=split,
            in_specs=placed,
            out_specs=(P(None, ROW, BAND), P(None, ROW, BAND)),
            check_vma=False,
        )(observed, row_taps, col_taps, spectral_basis, ridge_weights)

    return whole
```

time: 593 us -> 368 us (0.62); the launches traced: 582 us -> 367 us
  other arithmetic: 155 us -> 24.9 us
  blocking collectives: 196 us -> 88.6 us
  Pallas kernels: 0 us -> 93.3 us
  local copies, waits for them, and re-layouts: 125 us -> 63.5 us
  waiting for transfers between devices: 60.2 us -> 46.2 us
  between operations: 7.62 us -> 20.8 us
  matrix products: 10.7 us -> 0 us
    all_to_all x5 -> x0, blocking collectives: 127 us -> none  [the longest x3 68.2 us: to_subspace(): lax.all_to_all(band_field, BAND, split_axis=2, concat_axis=0, tiled=True)]
    convert_element_type x5 -> x1, other arithmetic: 96.1 us -> 0.01 us  [local(): eye = jnp.eye(8, dtype=BF)]
    pallas_call x0 -> x4, Pallas kernels: none -> 93.3 us  [the longest x2 43.3 us: normal(): call(functools.partial(normal_kernel, sizes), jax.ShapeDtypeStruct((comps...]
    add x5 -> x0, other arithmetic: 58.3 us -> none  [pass_rows(): running + kernel[:, offset, None, None] * padded[:, offset:offset + lengt...]
    ppermute x10, waiting for transfers between devices: 60.2 us -> 11.3 us  [shifted(): return lax.ppermute(x, axis, pairs)]
    unnamed x45 -> x19, local copies, waits for them, and re-layouts: 49.8 us -> 2.12 us
    mul x0 -> x5, local copies, waits for them, and re-layouts: none -> 46.9 us  [the longest x2 21.9 us: local(): basis.T[:, None, :, None] * eye[None, :, None, :]]
    all_to_all x7 -> x0, local copies, waits for them, and re-layouts: 35.3 us -> none  [the longest x3 24 us: to_subspace(): lax.all_to_all(band_field, BAND, split_axis=2, concat_axis=0, tiled=True)]
  transfers between devices with their start and end apart: 10 -> 11, of which waited for: 10 -> 7; matrix products, arithmetic and copies ran while one was open for 1% -> 18% of each run, Pallas kernels for 0% -> 11%
where the time goes in v1:
time: 368 us; the launch traced here: 367 us
  Pallas kernels  93.3 us (25%)
  blocking collectives  88.6 us (24%)
  local copies, waits for them, and re-layouts  63.5 us (17%)
  waiting for transfers between devices  46.2 us (13%)
  starting transfers between devices  29.2 us (8%)
  other arithmetic  24.9 us (7%)
  between operations  20.8 us (6%)
    psum x1, blocking collectives, local(): lax.psum(jnp.stack([jnp.sum(rhs * rhs), jnp.sum(rhs * q), jnp.sum(q * q),...  71.6 us
    pallas_call x2, Pallas kernels, normal(): call(functools.partial(normal_kernel, sizes), jax.ShapeDtypeStruct((comps...  43.3 us
    pallas_call x1, Pallas kernels, local(): call(functools.partial(normal_build_kernel, sizes), (jax.ShapeDtypeStruct...  38.9 us
    reduce_scatter x1, waiting for transfers between devices, local(): rhs = lax.psum_scatter(partial, BAND, scatter_dimension=0, tiled=True)[0]  34.9 us
    ppermute x10, starting transfers between devices, shifted(): return lax.ppermute(x, axis, pairs)  29.2 us
    mul x2, local copies, waits for them, and re-layouts, local(): basis.T[:, None, :, None] * eye[None, :, None, :]  21.9 us
    mul x1, local copies, waits for them, and re-layouts, local(): basis[:, None, :, None] * eye[None, :, None, :]  21.2 us
    all_gather x1, blocking collectives, local(): every = lax.all_gather(both, BAND, axis=0, tiled=True)  17 us
  transfers between devices with their start and end apart: 11, of which 7 were waited for; matrix products, arithmetic and copies ran while one was open for 18% of the time, Pallas kernels for 11%

profile of v1, /device:TPU:1, one launch (start us, length us, event | category | flops | bytes accessed | tf_op | source)
XLA Modules:
  0.0 366.7 jit_solution(8755548837283385804)
XLA Ops:
  12.0 5.8 %collective-permute-start = (bf16[28,12,680]{2,0,1:T(8,128)(2,1)}, bf16[28,12,680]{2,0,1:T(8,128)(2,1)}, u32[]{:S(2)}, u32[]{:S(2)}) collective-permute-start(bf16[28,12,680]{2,0,1:T(8,128)(2,1)} %copy.42), channel_id=1, source_target_pairs={{0,1},{1,2},{2,3},{3,4},{4,5},{5,6},{6,7},{7,8},{8,9},{9,10},{10,1... | collective-permute-start | bytes 1370888 | tf_op jit(solution)/shard_map/ppermute | solution.py:203
  18.5 3.0 mul.138
  23.0 4.4 %collective-permute-done.1 = bf16[28,12,680]{2,0,1:T(8,128)(2,1)} collective-permute-done((bf16[28,12,680]{2,0,1:T(8,128)(2,1)}, bf16[28,12,680]{2,0,1:T(8,128)(2,1)}, u32[]{:S(2)}, u32[]{:S(2)}) %collective-permute-start.1) | collective-permute-done | bytes 456992 | tf_op jit(solution)/shard_map/ppermute | solution.py:203
  30.7 2.1 fusion.14.obs_ref
  32.8 11.2 %shard_map.68 = f32[8,32,32,128]{3,2,1,0:T(8,128)} custom-call(bf16[28,56,768]{2,1,0:T(8,128)(2,1)} %fusion.14.obs_ref, f32[28,8,256]{2,1,0:T(8,128)} %pad.24.taps_ref, bf16[256,224]{1,0:T(8,128)(2,1)} %copy.28.p8_ref), custom_call_target="tpu_custom_call" | custom-call | flops 2000000000 | bytes 16777216 | tf_op jit(solution)/shard_map/pallas_call | solution.py:243
  44.3 6.2 %broadcast_multiply_fusion = bf16[32,8,225,8]{1,0,3,2:T(8,128)(2,1)} fusion(bf16[8,8]{0,1:T(8,128)(2,1)S(1)} %fusion.26, bf16[32,225]{0,1:T(8,128)(2,1)S(1)} %copy.35), kind=kLoop, calls=%fused_computation | loop fusion | flops 460800 | bytes 936128 | tf_op jit(solution)/shard_map/mul | solution.py:227
  50.5 34.9 %reduce-scatter.2.cloned.1.call-done = f32[1,32,32,128]{3,2,1,0:T(8,128)} async-done(((f32[8,32,32,128]{3,2,1,0:T(8,128)}), f32[1,32,32,128]{3,2,1,0:T(8,128)}) %reduce-scatter.2.cloned.1.call-update) | async-done | bytes 524304 | tf_op jit(solution)/shard_map/reduce_scatter | solution.py:254
  87.8 4.2 %collective-permute-start.2 = (bf16[32,24,85]{2,1,0:T(8,128)(2,1)S(1)}, bf16[32,24,85]{2,1,0:T(8,128)(2,1)S(1)}, u32[]{:S(2)}, u32[]{:S(2)}) collective-permute-start(bf16[32,24,85]{2,1,0:T(8,128)(2,1)S(1)} %get-tuple-element.21), channel_id=1, source_target_pairs={{0,1},{1,2},{2,3},{3,4},{4,5},{5,6},{6,7},{7,8},{8,9},{9,10},{10,1... | collective-permute-start | bytes 391688 | tf_op jit(solution)/shard_map/ppermute | solution.py:203
  92.0 6.2 %broadcast_multiply_fusion.1 = bf16[225,8,32,8]{3,2,1,0:T(8,128)(2,1)} fusion(bf16[8,8]{1,0:T(8,128)(2,1)S(1)} %copy.34, bf16[225,32]{1,0:T(8,128)(2,1)S(1)} %pad.26.clone), kind=kLoop, calls=%fused_computation.1 | loop fusion | flops 460800 | bytes 936128 | tf_op jit(solution)/shard_map/mul | solution.py:226
  98.2 21.2 %mul.143.e8_ref = bf16[1800,256]{1,0:T(8,128)(2,1)} reshape(bf16[225,8,32,8]{3,2,1,0:T(8,128)(2,1)} %broadcast_multiply_fusion.1) | data formatting | bytes 1843200 | tf_op jit(solution)/shard_map/mul | solution.py:226
  119.5 20.5 %mul.147 = bf16[256,1800]{0,1:T(8,128)(2,1)S(1)} reshape(bf16[32,8,225,8]{1,0,3,2:T(8,128)(2,1)} %broadcast_multiply_fusion) | data formatting | bytes 1843200 | tf_op jit(solution)/shard_map/mul | solution.py:227
  141.4 17.0 %all_gather.3 = f32[224,4,25]{2,1,0:T(4,128)S(1)} all-gather(f32[28,4,25]{2,1,0:T(4,128)S(1)} %pad_maximum_fusion.2), channel_id=1, replica_groups=mesh['band_0'=4,'band_1'=2,'row_0'=4,'row_1'=4] {'band_0','band_1'}, dimensions={0}, use_global_device_ids=true | all-gather | bytes 100800 | tf_op jit(solution)/shard_map/all_gather | solution.py:221
  160.5 2.1 collective-permute-start.5
  162.8 3.5 collective-permute-start.4
  166.3 38.9 %shard_map.69 = (bf16[225,144,128]{2,1,0:T(8,128)(2,1)}, bf16[75,96,256]{2,1,0:T(8,128)(2,1)}) custom-call(f32[225,8,256]{2,1,0:T(8,128)} %pad.27.taps_ref), custom_call_target="tpu_custom_call" | custom-call | flops 2000000000 | bytes 16777216 | tf_op jit(solution)/shard_map/pallas_call | solution.py:232
  205.9 2.2 fusion.16.pe_ref
  208.9 21.6 %shard_map.70.p_ref = f32[32,32,128]{2,1,0:T(8,128)} custom-call(bf16[32,80,256]{2,1,0:T(8,128)(2,1)} %fusion.16.pe_ref, bf16[1800,256]{1,0:T(8,128)(2,1)} %mul.143.e8_ref, bf16[256,1800]{1,0:T(8,128)(2,1)} %copy.36.p8_ref, bf16[225,144,128]{2,1,0:T(8,128)(2,1)} %get-tuple-element.4.tt_ref, bf16[75,96,256]{2,1,0:T(8,128)(2,1)} %get-tuple-element.5.rr_ref, ...), custom_call_target="tpu_custom_call" | custom-call | flops 20000000000 | bytes 16777216 | tf_op jit(solution)/shard_map/pallas_call | solution.py:265
  232.9 4.0 %collective-permute-start.6 = (bf16[32,24,85]{2,1,0:T(8,128)(2,1)S(1)}, bf16[32,24,85]{2,1,0:T(8,128)(2,1)S(1)}, u32[]{:S(2)}, u32[]{:S(2)}) collective-permute-start(bf16[32,24,85]{2,1,0:T(8,128)(2,1)S(1)} %get-tuple-element.19), channel_id=1, source_target_pairs={{0,1},{1,2},{2,3},{3,4},{4,5},{5,6},{6,7},{7,8},{8,9},{9,10},{10,1... | collective-permute-start | bytes 391688 | tf_op jit(solution)/shard_map/ppermute | solution.py:203
  236.9 2.6 collective-permute-done.7
  244.1 3.8 %collective-permute-start.8 = (bf16[32,80,24]{1,2,0:T(8,128)(2,1)S(1)}, bf16[32,80,24]{1,2,0:T(8,128)(2,1)S(1)}, u32[]{:S(2)}, u32[]{:S(2)}) collective-permute-start(bf16[32,80,24]{1,2,0:T(8,128)(2,1)S(1)} %copy.37), channel_id=1, source_target_pairs={{0,16},{16,32},{32,48},{48,64},{64,80},{80,96},{96,112},{1,17},{17... | collective-permute-start | bytes 368648 | tf_op jit(solution)/shard_map/ppermute | solution.py:203
  250.7 2.2 fusion.20.pe_ref
  252.9 21.7 %shard_map.71 = f32[32,32,128]{2,1,0:T(8,128)} custom-call(bf16[32,80,256]{2,1,0:T(8,128)(2,1)} %fusion.20.pe_ref, bf16[1800,256]{1,0:T(8,128)(2,1)} %mul.143.e8_ref, bf16[256,1800]{1,0:T(8,128)(2,1)} %copy.36.p8_ref, bf16[225,144,128]{2,1,0:T(8,128)(2,1)} %get-tuple-element.4.tt_ref, bf16[75,96,256]{2,1,0:T(8,128)(2,1)} %get-tuple-element.5.rr_ref, ...), custom_call_target="tpu_custom_call" | custom-call | flops 20000000000 | bytes 16777216 | tf_op jit(solution)/shard_map/pallas_call | solution.py:265
  276.5 3.2 stack.43
  279.8 71.6 %psum.7 = f32[5]{0:T(128)S(1)} all-reduce(f32[5]{0:T(128)S(1)} %stack.43), channel_id=1, replica_groups=mesh['band_0'=4,'band_1'=2,'row_0'=4,'row_1'=4] {'band_0','band_1','row_..., use_global_device_ids=true, to_apply=%region_6.7 | all-reduce | flops 5 | bytes 40 | tf_op jit(solution)/shard_map/psum | solution.py:280
  (76 shorter events, 31.7 us)
Async XLA Ops:
  7.2 10.6 %copy-start.5 = (f32[28,25]{1,0:T(8,128)S(1)}, f32[28,25]{1,0:T(8,128)}, u32[]{:S(2)}) copy-start(f32[28,25]{1,0:T(8,128)} %param.6) | copy-start | bytes 8404
  7.2 10.8 %copy-start.6 = (f32[28,25]{1,0:T(8,128)S(1)}, f32[28,25]{1,0:T(8,128)}, u32[]{:S(2)}) copy-start(f32[28,25]{1,0:T(8,128)} %param.7) | copy-start | bytes 8404
  7.2 10.9 %copy-start.4 = (bf16[224,32]{0,1:T(8,128)(2,1)S(1)}, bf16[224,32]{0,1:T(8,128)(2,1)}, u32[]{:S(2)}) copy-start(bf16[224,32]{0,1:T(8,128)(2,1)} %param.8) | copy-start | bytes 43012
  7.2 78.2 %reduce-scatter.2.cloned.1.call-start = ((), (), s32[]{:S(2)}) async-start(), calls=%async_computation.1 | async-start | bytes 4718592 | tf_op jit(solution)/shard_map/reduce_scatter | solution.py:254
  9.7 17.7 %collective-permute-start.1 = (bf16[28,12,680]{2,0,1:T(8,128)(2,1)}, bf16[28,12,680]{2,0,1:T(8,128)(2,1)}, u32[]{:S(2)}, u32[]{:S(2)}) collective-permute-start(bf16[28,12,680]{2,0,1:T(8,128)(2,1)} %copy.43), channel_id=1, source_target_pairs={{1,0},{2,1},{3,2},{4,3},{5,4},{6,5},{7,6},{8,7},{9,8},{10,9},{11,1... | collective-permute-start | bytes 1370888 | tf_op jit(solution)/shard_map/ppermute | solution.py:203
  12.0 17.3 %collective-permute-start = (bf16[28,12,680]{2,0,1:T(8,128)(2,1)}, bf16[28,12,680]{2,0,1:T(8,128)(2,1)}, u32[]{:S(2)}, u32[]{:S(2)}) collective-permute-start(bf16[28,12,680]{2,0,1:T(8,128)(2,1)} %copy.42), channel_id=1, source_target_pairs={{0,1},{1,2},{2,3},{3,4},{4,5},{5,6},{6,7},{7,8},{8,9},{9,10},{10,1... | collective-permute-start | bytes 1370888 | tf_op jit(solution)/shard_map/ppermute | solution.py:203
  18.5 12.2 %copy-start.1 = (bf16[28,32,680]{2,1,0:T(8,128)(2,1)S(1)}, bf16[28,32,680]{2,1,0:T(8,128)(2,1)}, u32[]{:S(2)}) copy-start(bf16[28,32,680]{2,1,0:T(8,128)(2,1)} %param.5) | copy-start | bytes 3655684
  86.5 73.3 %collective-permute-start.3 = (bf16[32,24,85]{2,1,0:T(8,128)(2,1)S(1)}, bf16[32,24,85]{2,1,0:T(8,128)(2,1)S(1)}, u32[]{:S(2)}, u32[]{:S(2)}) collective-permute-start(bf16[32,24,85]{2,1,0:T(8,128)(2,1)S(1)} %get-tuple-element.22), channel_id=1, source_target_pairs={{1,0},{2,1},{3,2},{4,3},{5,4},{6,5},{7,6},{8,7},{9,8},{10,9},{11,1... | collective-permute-start | bytes 391688 | tf_op jit(solution)/shard_map/ppermute | solution.py:203
  87.8 72.0 %collective-permute-start.2 = (bf16[32,24,85]{2,1,0:T(8,128)(2,1)S(1)}, bf16[32,24,85]{2,1,0:T(8,128)(2,1)S(1)}, u32[]{:S(2)}, u32[]{:S(2)}) collective-permute-start(bf16[32,24,85]{2,1,0:T(8,128)(2,1)S(1)} %get-tuple-element.21), channel_id=1, source_target_pairs={{0,1},{1,2},{2,3},{3,4},{4,5},{5,6},{6,7},{7,8},{8,9},{9,10},{10,1... | collective-permute-start | bytes 391688 | tf_op jit(solution)/shard_map/ppermute | solution.py:203
  160.5 44.7 %collective-permute-start.5 = (bf16[32,80,24]{1,2,0:T(8,128)(2,1)S(1)}, bf16[32,80,24]{1,2,0:T(8,128)(2,1)S(1)}, u32[]{:S(2)}, u32[]{:S(2)}) collective-permute-start(bf16[32,80,24]{1,2,0:T(8,128)(2,1)S(1)} %copy.30), channel_id=1, source_target_pairs={{16,0},{32,16},{48,32},{64,48},{80,64},{96,80},{112,96},{17,1},{33... | collective-permute-start | bytes 368648 | tf_op jit(solution)/shard_map/ppermute | solution.py:203
  162.8 42.7 %collective-permute-start.4 = (bf16[32,80,24]{1,2,0:T(8,128)(2,1)S(1)}, bf16[32,80,24]{1,2,0:T(8,128)(2,1)S(1)}, u32[]{:S(2)}, u32[]{:S(2)}) collective-permute-start(bf16[32,80,24]{1,2,0:T(8,128)(2,1)S(1)} %copy.29), channel_id=1, source_target_pairs={{0,16},{16,32},{32,48},{48,64},{64,80},{80,96},{96,112},{1,17},{17... | collective-permute-start | bytes 368648 | tf_op jit(solution)/shard_map/ppermute | solution.py:203
  205.2 2.9 copy-start.7
  231.6 7.9 %collective-permute-start.7 = (bf16[32,24,85]{2,1,0:T(8,128)(2,1)S(1)}, bf16[32,24,85]{2,1,0:T(8,128)(2,1)S(1)}, u32[]{:S(2)}, u32[]{:S(2)}) collective-permute-start(bf16[32,24,85]{2,1,0:T(8,128)(2,1)S(1)} %get-tuple-element.20), channel_id=1, source_target_pairs={{1,0},{2,1},{3,2},{4,3},{5,4},{6,5},{7,6},{8,7},{9,8},{10,9},{11,1... | collective-permute-start | bytes 391688 | tf_op jit(solution)/shard_map/ppermute | solution.py:203
  232.9 8.4 %collective-permute-start.6 = (bf16[32,24,85]{2,1,0:T(8,128)(2,1)S(1)}, bf16[32,24,85]{2,1,0:T(8,128)(2,1)S(1)}, u32[]{:S(2)}, u32[]{:S(2)}) collective-permute-start(bf16[32,24,85]{2,1,0:T(8,128)(2,1)S(1)} %get-tuple-element.19), channel_id=1, source_target_pairs={{0,1},{1,2},{2,3},{3,4},{4,5},{5,6},{6,7},{7,8},{8,9},{9,10},{10,1... | collective-permute-start | bytes 391688 | tf_op jit(solution)/shard_map/ppermute | solution.py:203
  241.9 7.0 %collective-permute-start.9 = (bf16[32,80,24]{1,2,0:T(8,128)(2,1)S(1)}, bf16[32,80,24]{1,2,0:T(8,128)(2,1)S(1)}, u32[]{:S(2)}, u32[]{:S(2)}) collective-permute-start(bf16[32,80,24]{1,2,0:T(8,128)(2,1)S(1)} %copy.38), channel_id=1, source_target_pairs={{16,0},{32,16},{48,32},{64,48},{80,64},{96,80},{112,96},{17,1},{33... | collective-permute-start | bytes 368648 | tf_op jit(solution)/shard_map/ppermute | solution.py:203
  244.1 6.2 %collective-permute-start.8 = (bf16[32,80,24]{1,2,0:T(8,128)(2,1)S(1)}, bf16[32,80,24]{1,2,0:T(8,128)(2,1)S(1)}, u32[]{:S(2)}, u32[]{:S(2)}) collective-permute-start(bf16[32,80,24]{1,2,0:T(8,128)(2,1)S(1)} %copy.37), channel_id=1, source_target_pairs={{0,16},{16,32},{32,48},{48,64},{64,80},{80,96},{96,112},{1,17},{17... | collective-permute-start | bytes 368648 | tf_op jit(solution)/shard_map/ppermute | solution.py:203
  252.9 21.7 %copy-start = (f32[32,32,128]{2,1,0:T(8,128)S(1)}, f32[32,32,128]{2,1,0:T(8,128)}, u32[]{:S(2)}) copy-start(f32[32,32,128]{2,1,0:T(8,128)} %shard_map.70.p_ref) | copy-start | bytes 1572868
  252.9 21.7 %copy-start.2 = (f32[1,32,32,128]{3,2,1,0:T(8,128)S(1)}, f32[1,32,32,128]{3,2,1,0:T(8,128)}, u32[]{:S(2)}) copy-start(f32[1,32,32,128]{3,2,1,0:T(8,128)} %reduce-scatter.2.cloned.1.call-done) | copy-start | bytes 1572868
  274.6 84.0 %copy-start.3 = (f32[32,32,128]{2,1,0:T(8,128)S(1)}, f32[32,32,128]{2,1,0:T(8,128)}, u32[]{:S(2)}) copy-start(f32[32,32,128]{2,1,0:T(8,128)} %shard_map.71) | copy-start | bytes 1572868
Sparse Core Ops, SparseCore 0:
  44.1 41.2 reduce-scatter.1

commit v2 on v0

v2 whole, which is shorter than its diff:
```python
import functools

import jax
import jax.numpy as jnp
from jax import lax
from jax.experimental import pallas as pl
from jax.experimental.pallas import tpu as pltpu
from jax.sharding import Mesh
from jax.sharding import PartitionSpec as P

AXES = ("band_0", "band_1", "row_0", "row_1")
BAND = ("band_0", "band_1")
ROW = ("row_0", "row_1")
TAPS = 25
RAD = 12
HALO = 24
LANES = 128
SLOT = 64
BF = jnp.bfloat16
F32 = jnp.float32


def iota(shape, dim):
    return lax.broadcasted_iota(jnp.int32, shape, dim)


def mm(a, b):
    return lax.dot_general(a, b, (((1,), (0,)), ((), ())), preferred_element_type=F32)


def onehot(mask):
    return jnp.where(mask, 1.0, 0.0)


def staircase(line, rows, shift):
    step = pltpu.roll(jnp.broadcast_to(line, (8, LANES)), 0, 1, stride=1, stride_axis=0)
    tiles = []
    for g in range(rows // 8):
        turn = (shift + 8 * g) % LANES
        tiles.append(pltpu.roll(step, turn, 1) if turn else step)
    return jnp.concatenate(tiles, axis=0)


def kernel(
    dims, obs, edges, feats, taps, basis, basis_t, ridge,
    out_x, out_r,
    edge_in, line_in, lines, rows_adj, cols_adj, zed, keep, out_a, in_a, out_b, in_b,
    tt, rr, e8, p8, p8_own, spec, mid, fin, work, ext, pack, pack_in, vec, red_src, red_in,
    edge_sem, line_sem, a_sem, b_sem, row_sem, col_sem, red_sem,
):
    cols, sizes = dims
    ny, nc, nx, nz = sizes
    nbd, nrow = ny * nc, nx * nz
    y, core = lax.axis_index("band_0"), lax.axis_index("band_1")
    x, z = lax.axis_index("row_0"), lax.axis_index("row_1")
    j, i_row = y * nc + core, x * nz + z
    own, rows, full = obs.shape
    bands, comps = basis.shape
    ext_r = rows + 2 * HALO
    nblk, next_ = rows // 8, ext_r // 8
    ck = comps * 8
    ku = tt.shape[1]
    first, last = j == 0, j == nbd - 1
    top_dev, low_dev = i_row == 0, i_row == nrow - 1

    def at_band(jj):
        return (jj // nc, lax.rem(jj, nc), x, z)

    def at_row(ii):
        return (y, core, ii // nz, lax.rem(ii, nz))

    up = at_row(lax.rem(i_row + nrow - 1, nrow))
    down = at_row(lax.rem(i_row + 1, nrow))
    left = at_band(lax.rem(j + nbd - 1, nbd))
    right = at_band(lax.rem(j + 1, nbd))
    partner = (y, 1 - core, x, z)
    peers = [at_band(lax.rem(j + s, nbd)) for s in range(1, nbd)]
    peers_x = [(y, core, lax.rem(x + s, nx), z) for s in range(1, nx)]
    peers_z = [(y, core, x, lax.rem(z + s, nz)) for s in range(1, nz)]

    barrier = pltpu.get_barrier_semaphore()
    everyone = [up, down] + peers + peers_x + peers_z
    for d in everyone:
        pl.semaphore_signal(barrier, inc=1, device_id=d, device_id_type=pl.DeviceIdType.MESH)
    pl.semaphore_wait(barrier, len(everyone))

    def remote(src, dst, send, recv, device):
        return pltpu.make_async_remote_copy(
            src_ref=src, dst_ref=dst, send_sem=send, recv_sem=recv,
            device_id=device, device_id_type=pl.DeviceIdType.MESH,
        )

    to_up = remote(edges.at[0], edge_in.at[1], edge_sem.at[0], edge_sem.at[2], up)
    to_down = remote(edges.at[1], edge_in.at[0], edge_sem.at[1], edge_sem.at[3], down)
    to_up.start()
    to_down.start()

    line_copies = []
    row_kind = jnp.where(low_dev, 3, 2)
    for s in range(1, nbd):
        dest = lax.rem(j + s, nbd)
        for k, kind in enumerate((jnp.where(dest == nbd - 1, 1, 0), row_kind)):
            c = remote(
                feats.at[kind], line_in.at[j, k], line_sem.at[0, s - 1, k], line_sem.at[1, s - 1, k], at_band(dest)
            )
            c.start()
            line_copies.append(c)
    line_in[j, 0] = feats[jnp.where(last, 1, 0)]
    line_in[j, 1] = feats[row_kind]

    r, l = iota((rows, LANES), 0), iota((rows, LANES), 1)

    def own_rows(g, carry):
        for q in range(4):
            line = taps[4 * g + q][1:2]
            d = l - rows * q + RAD - r
            m = (d >= 0) & (d < TAPS) & (l >= rows * q) & (l < rows * (q + 1))
            mine = jnp.where(m, staircase(line, rows, rows * q - RAD), 0.0)
            k = l - RAD * q
            d = k - r
            m = (d >= 0) & (d < TAPS) & (k >= 0) & (k < RAD)
            above = jnp.where(m, staircase(line, rows, RAD * q), 0.0)
            k = l - 4 * RAD - RAD * q
            d = k + rows + RAD - r
            m = (d >= 0) & (d < TAPS) & (k >= 0) & (k < RAD)
            below = jnp.where(m, staircase(line, rows, 4 * RAD + RAD * q - RAD - rows), 0.0)
            rows_adj[g, rows * q : rows * (q + 1), :LANES] = mine.astype(BF)
            rows_adj[g, rows * q : rows * (q + 1), LANES:] = (above + below).astype(BF)
        return carry

    lax.fori_loop(0, own // 4, own_rows, 0)

    kw = cols_adj.shape[1]
    w, o = iota((kw, LANES), 0), iota((kw, LANES), 1)

    def own_cols(b, carry):
        line = taps[b][0:1]
        for k in range(2):
            d = w - o - cols * k
            m = (d >= 0) & (d < TAPS) & (o < cols)
            t = jnp.where(m, staircase(line, kw, -HALO - cols * k), 0.0)
            cols_adj[b, :, LANES * k : LANES * (k + 1)] = t.astype(BF)
        return carry

    lax.fori_loop(0, own, own_cols, 0)

    spread = onehot(iota((comps, ck), 0) == (iota((comps, ck), 1) >> 3)).astype(BF)
    wide = mm(basis[...], spread)
    step = bands // 4
    er, el = iota((8 * step, ck), 0), iota((8 * step, ck), 1)
    for c in range(4):
        v = jnp.broadcast_to(wide[step * c : step * (c + 1)][:, None, :], (step, 8, ck)).reshape(8 * step, ck)
        e8[8 * step * c : 8 * step * (c + 1)] = jnp.where((er & 7) == (el & 7), v, 0.0).astype(BF)
    tall = onehot(iota((ck, comps), 1) == (iota((ck, comps), 0) >> 3)).astype(BF)
    tall = mm(tall, basis_t[...]).astype(BF)
    br, bl = iota((256, 256), 0), iota((256, 256), 1)
    same = (br & 7) == (bl & 7)

    def widen(start):
        return jnp.where(same, mm(tall, onehot(br == start + (bl >> 3)).astype(BF)), 0.0).astype(BF)

    for c in range(bands // 32):
        p8[:, 256 * c : 256 * (c + 1)] = widen(32 * c)
    p8_own[...] = widen(own * j)

    for c in line_copies:
        c.wait()
    for k in range(2):
        for jj in range(nbd):
            lines[k, own * jj : own * (jj + 1)] = line_in[jj, k][:own].astype(F32)
    groups = bands // 8
    wide_n = 16 * LANES

    def shifted(depth, hit, edge_hit):
        f, n = iota((depth, wide_n), 0), iota((depth, wide_n), 1)
        s = onehot(f == hit(n))
        if edge_hit is not None:
            s = s - onehot(f == edge_hit(n))
        return s.astype(BF)

    def unfold(k, depth, sel):
        res = mm(lines[k, :, :depth].astype(BF), sel)
        for t in range(16):
            work[:, 8 * t : 8 * (t + 1), :] = res[:, LANES * t : LANES * (t + 1)].reshape(groups, 8, LANES)

    def tt_pair(p, carry, depth):
        def hit(n):
            a, b = 16 * p + (n >> 7), n & 127
            return jnp.where((b < cols) & (a < cols + 2 * HALO) & (a - b <= 2 * HALO), a - b, -1)

        def edge_hit(n):
            a, b = 16 * p + (n >> 7) - HALO, n & 127
            a, b = jnp.where(last, cols - 1 - a, a), jnp.where(last, cols - 1 - b, b)
            ok = (first | last) & (a >= 0) & (a < RAD) & (b >= 0) & (b < RAD)
            return jnp.where(ok, SLOT + RAD * a + b, -1)

        unfold(0, depth, shifted(depth, hit, edge_hit if depth > SLOT else None))

        def place(g, c):
            for s in range(8):
                v = work[g, pl.ds(s, 16, stride=8), :]
                tt[8 * g + s, pl.ds(pl.multiple_of(16 * p, 16), 16), :] = v.astype(BF)
            return c

        lax.fori_loop(0, groups, place, 0)
        return carry

    lax.fori_loop(0, ku // 16, functools.partial(tt_pair, depth=SLOT), 0)

    @pl.when(first | last)
    def _():
        p0 = jnp.where(first, HALO // 16, (cols + RAD - 1) // 16)
        lax.fori_loop(p0, p0 + 2, functools.partial(tt_pair, depth=256), 0)

    third = rr.shape[0]
    lane16 = iota((16, LANES), 1)

    def rr_pair(p, carry):
        def hit(n):
            a, b = 16 * p + (n >> 7), n & 127
            return jnp.where((b < ext_r) & (b >= a) & (b - a <= 2 * HALO), b - a, -1)

        def edge_hit(n):
            a, b = 16 * p + (n >> 7), (n & 127) - HALO
            a, b = jnp.where(low_dev, rows - 1 - a, a), jnp.where(low_dev, rows - 1 - b, b)
            ok = (top_dev | low_dev) & (a >= 0) & (a < RAD) & (b >= 0) & (b < RAD)
            return jnp.where(ok, SLOT + RAD * a + b, -1)

        unfold(1, 256, shifted(256, hit, edge_hit))
        for q in range(3):
            lo = ext_r * q

            def place(g, c):
                for s in range(8):
                    v = work[g, pl.ds(s, 16, stride=8), :]
                    if lo % LANES:
                        v = pltpu.roll(v, lo % LANES, 1)
                    t0 = v if lo + ext_r <= LANES else jnp.where(lane16 >= lo, v, 0.0)
                    t1 = v if lo >= LANES else jnp.where(lane16 < lo + ext_r - LANES, v, 0.0)
                    at = (8 * g + s - third * q, pl.ds(pl.multiple_of(rows * q + 16 * p, 16), 16))
                    rr[at + (slice(0, LANES),)] = t0.astype(BF)
                    rr[at + (slice(LANES, 2 * LANES),)] = t1.astype(BF)
                return c

            lax.fori_loop(third * q // 8, min(third * (q + 1), bands) // 8, place, 0)
        return carry

    lax.fori_loop(0, rows // 16, rr_pair, 0)

    to_up.wait()
    to_down.wait()
    above_ok, below_ok = i_row > 0, i_row < nrow - 1

    def adjoint(g, carry):
        e = pl.ds(pl.multiple_of(4 * RAD * g, 16), 4 * RAD)
        above = edge_in[0, e]
        below = edge_in[1, e]
        mine = obs[pl.ds(4 * g, 4)].reshape(4 * rows, full)
        above = jnp.where(above_ok, above, jnp.zeros_like(above))
        below = jnp.where(below_ok, below, jnp.zeros_like(below))
        v = mm(rows_adj[g][:, : 4 * rows + 8 * RAD], jnp.concatenate([mine, above, below], axis=0))
        wins = []
        for k in range(ny):
            start = nc * cols * k - RAD
            wins.append(pltpu.roll(v, (full - start) % full, 1)[:, :256].astype(BF))
        for q in range(4):
            u = jnp.concatenate([t[rows * q : rows * (q + 1)] for t in wins], axis=0)
            u = mm(u[:, :kw], cols_adj[4 * g + q])
            for k in range(ny):
                zed[k, 4 * g + q] = u[rows * k : rows * (k + 1)]
        return carry

    lax.fori_loop(0, own // 4, adjoint, 0)

    offsets = [s for s in (2, 1, 3, 0) if s < ny]
    a_copies, b_copies = [], []

    def merge(idx):
        a_copies[idx].wait()
        done = idx == len(offsets) - 1

        def add(i, carry):
            v = keep[idx, i] + in_a[idx, i].astype(F32)
            if done:
                vec[0, i] = v
            else:
                out_b[idx, i] = v.astype(BF)
            return carry

        lax.fori_loop(0, nblk, add, 0)
        if not done:
            dest = (lax.rem(y + offsets[idx], ny), core, x, z)
            c = remote(out_b.at[idx], in_b.at[idx], b_sem.at[0, idx], b_sem.at[1, idx], dest)
            c.start()
            b_copies.append(c)

    for idx, off in enumerate(offsets):
        k = lax.rem(y + off, ny)

        def project(i, carry):
            v = zed[k, :, pl.ds(pl.multiple_of(8 * i, 8), 8), :].reshape(own * 8, 256).astype(BF)
            v = mm(p8_own[:, : own * 8], v)
            lo, hi = v[:, :LANES], v[:, LANES:]
            keep[idx, i] = jnp.where(core == 0, lo, hi)
            out_a[idx, i] = jnp.where(core == 0, hi, lo).astype(BF)
            return carry

        lax.fori_loop(0, nblk, project, 0)
        c = remote(out_a.at[idx], in_a.at[idx], a_sem.at[0, idx], a_sem.at[1, idx], partner)
        c.start()
        a_copies.append(c)
        if idx:
            merge(idx - 1)
    merge(len(offsets) - 1)
    mid[pl.ds(bands, mid.shape[0] - bands)] = jnp.zeros((mid.shape[0] - bands, ext_r, LANES), BF)
    for idx, c in enumerate(b_copies):
        c.wait()

        def collect(i, carry):
            vec[0, i] = vec[0, i] + in_b[idx, i].astype(F32)
            return carry

        lax.fori_loop(0, nblk, collect, 0)

    chunk = ck // 4
    per = next_ // 2
    lane_c = iota((chunk, LANES), 1)
    lane_k = iota((ck, LANES), 1)

    def normal(n, carry):
        def stage(i, c):
            ext[n, 3 + i] = vec[n, i].astype(BF)
            return c

        lax.fori_loop(0, nblk, stage, 0)
        r_up = remote(ext.at[n, pl.ds(3, 3)], ext.at[n, pl.ds(3 + nblk, 3)], row_sem.at[n, 0], row_sem.at[n, 2], up)
        r_down = remote(ext.at[n, pl.ds(nblk, 3)], ext.at[n, pl.ds(0, 3)], row_sem.at[n, 1], row_sem.at[n, 3], down)
        r_up.start()
        r_down.start()
        r_up.wait()
        r_down.wait()

        def packing(c, cc):
            t, part = c // 4, lax.rem(c, 4)
            sl = pl.ds(pl.multiple_of(chunk * part, chunk), chunk)
            a = jnp.zeros((chunk, LANES), F32)
            b = a
            for g in range(per):
                v = ext[n, per * t + g, sl, :].astype(F32)
                m = (lane_c >= HALO * g) & (lane_c < HALO * (g + 1))
                a = jnp.where(m, pltpu.roll(v, HALO * g, 1) if g else v, a)
                b = jnp.where(m, pltpu.roll(v, (HALO * g - cols + HALO) % LANES, 1), b)
            pack[n, 0, t, sl, :] = a.astype(BF)
            pack[n, 1, t, sl, :] = b.astype(BF)
            return cc

        lax.fori_loop(0, 8, packing, 0)
        c_left = remote(pack.at[n, 0], pack_in.at[n, 1], col_sem.at[n, 0], col_sem.at[n, 2], left)
        c_right = remote(pack.at[n, 1], pack_in.at[n, 0], col_sem.at[n, 1], col_sem.at[n, 3], right)
        c_left.start()
        c_right.start()
        c_left.wait()
        c_right.wait()

        def block(blk):
            t, g = blk // per, lax.rem(blk, per)
            mine = pltpu.roll(ext[n, blk].astype(F32), HALO, 1)
            a = pltpu.roll(pack_in[n, 0, t].astype(F32), lax.rem(LANES - HALO * g, LANES), 1)
            b = pltpu.roll(pack_in[n, 1, t].astype(F32), lax.rem(2 * LANES + cols + HALO - HALO * g, LANES), 1)
            inside = jnp.logical_not((top_dev & (blk < 3)) | (low_dev & (blk >= 3 + nblk)))
            a_ok = inside & jnp.logical_not(first)
            b_ok = inside & jnp.logical_not(last)
            a = jnp.where(a_ok, a, 0.0)
            b = jnp.where(b_ok, b, 0.0)
            mine = jnp.where(inside, mine, 0.0)
            t0 = jnp.where(lane_k < HALO, a, jnp.where(lane_k < HALO + cols, mine, b))
            t1 = jnp.where(lane_k < cols + 2 * HALO - LANES, b, 0.0)
            return jnp.concatenate([t0, t1], axis=1).astype(BF)

        def expand(i, c):
            x0, x1 = block(2 * i), block(2 * i + 1)
            for m in range(4):
                e = e8[8 * step * m : 8 * step * (m + 1)]
                y0 = mm(e, x0).reshape(step, 8, 256)
                y1 = mm(e, x1).reshape(step, 8, 256)
                v = jnp.concatenate([y0, y1], axis=1).astype(BF)
                spec[step * m : step * (m + 1), pl.ds(pl.multiple_of(16 * i, 16), 16), :] = v
            return c

        lax.fori_loop(0, next_ // 2, expand, 0)

        def columns(g, c):
            for q in range(8):
                b = 8 * g + q
                mid[b] = mm(spec[b][:, :ku], tt[b]).astype(BF)
            return c

        lax.fori_loop(0, bands // 8, columns, 0)

        def along(g, c):
            for q in range(5):
                t = 5 * g + q
                v = jnp.concatenate([mid[t], mid[third + t], mid[2 * third + t]], axis=0)
                v = mm(rr[t][:, : 3 * ext_r], v)
                for k in range(3):
                    fin[third * k + t] = v[rows * k : rows * (k + 1)]
            return c

        lax.fori_loop(0, third // 5, along, 0)

        def project(i, c):
            v = fin[:bands, pl.ds(pl.multiple_of(8 * i, 8), 8), :].reshape(bands * 8, LANES).astype(BF)
            vec[n + 1, i] = mm(p8[...], v) + ridge[...] * vec[n, i]
            return c

        lax.fori_loop(0, nblk, project, 0)
        return carry

    lax.fori_loop(0, 2, normal, 0)

    def products(i, sums):
        a, b, c = vec[0, i], vec[1, i], vec[2, i]
        parts = [a * a, a * b, b * b, a * c, b * c]
        return tuple(s + jnp.sum(v.reshape(comps, 8, LANES), axis=0) for s, v in zip(sums, parts))

    zero = jnp.zeros((8, LANES), F32)
    sums = lax.fori_loop(0, nblk, products, (zero,) * 5)
    total = jnp.concatenate([jnp.sum(v, axis=0, keepdims=True) for v in sums] + [jnp.zeros((3, LANES), F32)], axis=0)
    at = 0
    for level, (group, place, count) in enumerate(((peers, j, nbd), (peers_x, x, nx), (peers_z, z, nz))):
        red_src[level] = total
        red_in[level, place] = total
        copies = []
        for d in group:
            c = remote(red_src.at[level], red_in.at[level, place], red_sem.at[0, at], red_sem.at[1, at], d)
            c.start()
            copies.append(c)
            at += 1
        for c in copies:
            c.wait()
        total = red_in[level, 0]
        for k in range(1, count):
            total = total + red_in[level, k]
    tot = jnp.sum(total, axis=1, keepdims=True)
    r00, r01, r11, r02, r12 = [tot[k : k + 1] for k in range(5)]
    alpha = r00 / r01
    new = r00 - 2.0 * alpha * r01 + alpha * alpha * r11
    gain = 1.0 + new / r00
    curve = gain * gain * r01 - alpha * gain * (r11 + r02) + alpha * alpha * r12
    alpha2 = new / curve

    def finish(i, carry):
        a, b, c = vec[0, i], vec[1, i], vec[2, i]
        xs = alpha * a + alpha2 * (gain * a - alpha * b)
        rs = (a - alpha * b) - alpha2 * (gain * b - alpha * c)
        sl = pl.ds(pl.multiple_of(8 * i, 8), 8)
        out_x[:, sl, :] = xs.reshape(comps, 8, LANES)[:, :, :cols]
        out_r[:, sl, :] = rs.reshape(comps, 8, LANES)[:, :, :cols]
        return carry

    lax.fori_loop(0, nblk, finish, 0)


def features(t):
    wide = jnp.pad(t, ((0, 0), (0, 0), (TAPS - 1, TAPS - 1)))
    auto = sum(t[:, :, m : m + 1] * wide[:, :, m : m + 2 * TAPS - 1] for m in range(TAPS))
    tail = jnp.pad(t[:, :, RAD + 1 :], ((0, 0), (0, 0), (0, RAD)))
    cut = 0.0
    for m in range(RAD):
        v = tail[:, :, m : m + RAD]
        cut = cut + v[:, :, :, None] * v[:, :, None, :]
    cut = cut.reshape(t.shape[0], t.shape[1], RAD * RAD)
    auto = jnp.pad(auto, ((0, 0), (0, 0), (0, SLOT - 2 * TAPS + 1)))
    both = jnp.concatenate([auto, cut], axis=2)
    return jnp.pad(both, ((0, 0), (0, -t.shape[1] % 16), (0, 256 - both.shape[2]))).astype(BF)


def local(height, width, sizes, observed, row_taps, col_taps, spectral_basis, ridge_weights):
    own, rows, _ = observed.shape
    bands, comps = spectral_basis.shape
    ny, nc, nx, nz = sizes
    nbd = ny * nc
    cols = width // nbd
    full = -(-width // LANES) * LANES
    ext_r = rows + 2 * HALO
    ck, nblk = comps * 8, rows // 8
    third = -(-bands // 24) * 8
    ku = -(-(cols + 2 * HALO) // 16) * 16
    kw = -(-(nc * cols + 2 * RAD) // 16) * 16

    obs = jnp.pad(observed, ((0, 0), (0, 0), (0, full - width)))
    edges = jnp.stack([obs[:, :RAD].reshape(own * RAD, full), obs[:, rows - RAD :].reshape(own * RAD, full)])
    feats = features(jnp.stack([col_taps, col_taps[:, ::-1], row_taps, row_taps[:, ::-1]]))
    taps = jnp.pad(jnp.stack([col_taps, row_taps[:, ::-1]], axis=1), ((0, 0), (0, 6), (0, LANES - TAPS)))
    basis_t = jnp.pad(spectral_basis.T, ((0, 0), (0, 256 - bands)))
    ridge = jnp.broadcast_to(jnp.repeat(ridge_weights, 8)[:, None], (ck, LANES))

    def vm(*shape, dtype=BF):
        return pltpu.VMEM(shape, dtype)

    dma = pltpu.SemaphoreType.DMA
    scratch = [
        vm(2, own * RAD, full),
        vm(nbd, 2, feats.shape[1], 256),
        vm(2, bands, 256, dtype=F32),
        vm(own // 4, 4 * rows, 256),
        vm(own, kw, 256),
        vm(ny, own, rows, 256, dtype=F32),
        vm(ny, nblk, ck, LANES, dtype=F32),
        vm(ny, nblk, ck, LANES),
        vm(ny, nblk, ck, LANES),
        vm(ny - 1, nblk, ck, LANES),
        vm(ny - 1, nblk, ck, LANES),
        vm(bands, ku, LANES),
        vm(third, 3 * rows, 256),
        vm(bands * 8, ck),
        vm(ck, bands * 8),
        vm(ck, 256),
        vm(bands, ext_r, 256),
        vm(3 * third, ext_r, LANES),
        vm(3 * third, rows, LANES, dtype=F32),
        vm(bands // 8, LANES, LANES, dtype=F32),
        vm(2, ext_r // 8, ck, LANES),
        vm(2, 2, 2, ck, LANES),
        vm(2, 2, 2, ck, LANES),
        vm(3, nblk, ck, LANES, dtype=F32),
        vm(3, 8, LANES, dtype=F32),
        vm(3, max(nbd, nx, nz), 8, LANES, dtype=F32),
        dma((4,)),
        dma((2, nbd - 1, 2)),
        dma((2, ny)),
        dma((2, ny - 1)),
        dma((2, 4)),
        dma((2, 4)),
        dma((2, nbd + nx + nz - 3)),
    ]
    shape = jax.ShapeDtypeStruct((comps, rows, cols), F32)
    vmem = pl.BlockSpec(memory_space=pltpu.VMEM)
    return pl.pallas_call(
        functools.partial(kernel, (cols, sizes)),
        out_shape=(shape, shape),
        in_specs=[vmem] * 7,
        out_specs=(vmem, vmem),
        scratch_shapes=scratch,
        compiler_params=pltpu.CompilerParams(
            collective_id=0, has_side_effects=True, vmem_limit_bytes=67043328
        ),
    )(obs, edges, feats, taps, spectral_basis, basis_t, ridge)


def solution(mesh):
    sizes = (4, 2, 4, 4)
    split = Mesh(mesh.devices.reshape(sizes), AXES)
    placed = (P(BAND, ROW, None), P(BAND, None), P(BAND, None), P(), P())

    def whole(observed, row_taps, col_taps, spectral_basis, ridge_weights):
        _, height, width = observed.shape
        return jax.shard_map(
            functools.partial(local, height, width, sizes),
            mesh=split,
            in_specs=placed,
            out_specs=(P(None, ROW, BAND), P(None, ROW, BAND)),
            check_vma=False,
        )(observed, row_taps, col_taps, spectral_basis, ridge_weights)

    return whole
```

time: 593 us -> 137 us (0.23); the launches traced: 582 us -> 136 us
  blocking collectives: 196 us -> 0 us
  other arithmetic: 155 us -> 4.03 us
  Pallas kernels: 0 us -> 117 us
  local copies, waits for them, and re-layouts: 125 us -> 13.9 us
  waiting for transfers between devices: 60.2 us -> 0 us
  starting transfers between devices: 27.2 us -> 0 us
  matrix products: 10.7 us -> 0 us
  between operations: 7.62 us -> 0.72 us
    all_to_all x5 -> x0, blocking collectives: 127 us -> none  [the longest x3 68.2 us: to_subspace(): lax.all_to_all(band_field, BAND, split_axis=2, concat_axis=0, tiled=True)]
    pallas_call x0 -> x1, Pallas kernels: none -> 117 us  [local(): pl.pallas_call(functools.partial(kernel, (cols, sizes)), out_shape=(shape...]
    convert_element_type x5 -> x0, other arithmetic: 96.1 us -> none  [the longest x2 38.5 us: normal_map(): pass_cols(pass_rows(padded, row_taps), col_taps).astype(jnp.bfloat16)]
    psum x8 -> x0, blocking collectives: 69.2 us -> none  [over_axes(): return functools.reduce(lax.psum, axes, value)]
    ppermute x10 -> x0, waiting for transfers between devices: 60.2 us -> none  [the longest x5 30.3 us: extended(): lax.ppermute(tail, axis, [(i, (i + 1) % count) for i in range(ends)])]
    add x5 -> x0, other arithmetic: 58.3 us -> none  [pass_rows(): running + kernel[:, offset, None, None] * padded[:, offset:offset + lengt...]
    unnamed x45 -> x9, local copies, waits for them, and re-layouts: 49.8 us -> 3.46 us
    all_to_all x7 -> x0, local copies, waits for them, and re-layouts: 35.3 us -> none  [the longest x3 24 us: to_subspace(): lax.all_to_all(band_field, BAND, split_axis=2, concat_axis=0, tiled=True)]
  transfers between devices with their start and end apart: 10 -> 0, of which waited for: 10 -> 0; matrix products, arithmetic and copies ran while one was open for 1% -> 0% of each run, Pallas kernels for 0% -> 0%
where the time goes in v2:
time: 137 us; the launch traced here: 136 us
  Pallas kernels  117 us (85%)
  local copies, waits for them, and re-layouts  13.9 us (10%)
  other arithmetic  4.03 us (3%)
    pallas_call x1, Pallas kernels, local(): pl.pallas_call(functools.partial(kernel, (cols, sizes)), out_shape=(shape...  117 us
    unnamed x9, local copies, waits for them, and re-layouts  3.46 us

profile of v2, /device:TPU:1, one launch (start us, length us, event | category | flops | bytes accessed | tf_op | source)
XLA Modules:
  0.0 135.8 jit_solution(2712266456237930130)
XLA Ops:
  0.6 0.7 copy.33
  1.4 0.8 rev.8
  2.2 0.7 broadcast_in_dim.6
  3.0 1.3 pad.36.basis_t
  4.3 0.8 rev.7
  5.1 0.7 pad_maximum_fusion.1
  5.9 0.3 slice_reduce_fusion.23
  6.2 0.8 slice_reduce_fusion.24
  7.0 0.9 add_convert_fusion.1
  8.1 0.7 copy.35.basis
  8.8 0.7 select_maximum_fusion.taps
  9.5 0.8 broadcast_in_dim.8.ridge
  10.3 0.2 pad_slice_fusion.10
  11.7 0.5 add_convert_fusion
  12.2 0.2 copy.32
  12.5 0.7 pad.34.feats
  13.1 1.2 pad.30.obs
  14.3 0.2 pad_slice_fusion.12
  14.6 0.1 stack_reshape.6
  14.7 0.1 stack_reshape.7
  14.8 1.1 pad_maximum_fusion.edges
  15.9 117.2 %shard_map.68 = (f32[32,32,85]{2,1,0:T(8,128)}, f32[32,32,85]{2,1,0:T(8,128)}) custom-call(bf16[28,32,768]{2,1,0:T(8,128)(2,1)} %pad.30.obs, bf16[2,336,768]{2,1,0:T(8,128)(2,1)} %pad_maximum_fusion.edges, bf16[4,32,256]{2,1,0:T(8,128)(2,1)} %pad.34.feats, f32[28,8,128]{2,1,0:T(8,128)} %select_maximum_fusion.taps, bf16[224,32]{1,0:T(8,128)(2,1)} %copy.35.basis, ...), custom_call_target="tpu_custom_call" | custom-call | tf_op jit(solution)/shard_map/pallas_call | solution.py:539
  133.1 1.9 %copy.38 = f32[32,32,85]{2,1,0:T(8,128)} copy(f32[32,32,85]{2,1,0:T(8,128)} %get-tuple-element.42) | data formatting | bytes 696320
  135.0 0.8 copy.39
  (22 shorter events, 1.6 us)
Async XLA Ops:
  0.6 7.4 %copy-start.2 = (bf16[224,32]{0,1:T(8,128)(2,1)S(1)}, bf16[224,32]{0,1:T(8,128)(2,1)}, u32[]{:S(2)}) copy-start(bf16[224,32]{0,1:T(8,128)(2,1)} %param.8) | copy-start | bytes 43012
  10.2 2.9 %copy-start = (bf16[28,32,680]{2,1,0:T(8,128)(2,1)S(1)}, bf16[28,32,680]{2,1,0:T(8,128)(2,1)}, u32[]{:S(2)}) copy-start(bf16[28,32,680]{2,1,0:T(8,128)(2,1)} %param.5) | copy-start | bytes 3655684
  133.1 1.9 %copy-start.1 = (f32[32,32,85]{2,1,0:T(8,128)S(1)}, f32[32,32,85]{2,1,0:T(8,128)}, u32[]{:S(2)}) copy-start(f32[32,32,85]{2,1,0:T(8,128)} %get-tuple-element.43) | copy-start | bytes 1044484

commit v3 on v2

--- a/solution.py
+++ b/solution.py
@@ -75,11 +75,10 @@
     right = at_band(lax.rem(j + 1, nbd))
     partner = (y, 1 - core, x, z)
     peers = [at_band(lax.rem(j + s, nbd)) for s in range(1, nbd)]
-    peers_x = [(y, core, lax.rem(x + s, nx), z) for s in range(1, nx)]
-    peers_z = [(y, core, x, lax.rem(z + s, nz)) for s in range(1, nz)]
+    peers_r = [at_row(lax.rem(i_row + s, nrow)) for s in range(1, nrow)]
 
     barrier = pltpu.get_barrier_semaphore()
-    everyone = [up, down] + peers + peers_x + peers_z
+    everyone = peers + peers_r
     for d in everyone:
         pl.semaphore_signal(barrier, inc=1, device_id=d, device_id_type=pl.DeviceIdType.MESH)
     pl.semaphore_wait(barrier, len(everyone))
@@ -204,13 +203,6 @@
 
         lax.fori_loop(0, groups, place, 0)
         return carry
-
-    lax.fori_loop(0, ku // 16, functools.partial(tt_pair, depth=SLOT), 0)
-
-    @pl.when(first | last)
-    def _():
-        p0 = jnp.where(first, HALO // 16, (cols + RAD - 1) // 16)
-        lax.fori_loop(p0, p0 + 2, functools.partial(tt_pair, depth=256), 0)
 
     third = rr.shape[0]
     lane16 = iota((16, LANES), 1)
@@ -312,6 +304,13 @@
         if idx:
             merge(idx - 1)
     merge(len(offsets) - 1)
+    lax.fori_loop(0, ku // 16, functools.partial(tt_pair, depth=SLOT), 0)
+
+    @pl.when(first | last)
+    def _():
+        p0 = jnp.where(first, HALO // 16, (cols + RAD - 1) // 16)
+        lax.fori_loop(p0, p0 + 2, functools.partial(tt_pair, depth=256), 0)
+
     mid[pl.ds(bands, mid.shape[0] - bands)] = jnp.zeros((mid.shape[0] - bands, ext_r, LANES), BF)
     for idx, c in enumerate(b_copies):
         c.wait()
@@ -363,11 +362,11 @@
         c_right.wait()
 
         def block(blk):
-            t, g = blk // per, lax.rem(blk, per)
+            t, g = blk // per, blk % per
             mine = pltpu.roll(ext[n, blk].astype(F32), HALO, 1)
-            a = pltpu.roll(pack_in[n, 0, t].astype(F32), lax.rem(LANES - HALO * g, LANES), 1)
-            b = pltpu.roll(pack_in[n, 1, t].astype(F32), lax.rem(2 * LANES + cols + HALO - HALO * g, LANES), 1)
-            inside = jnp.logical_not((top_dev & (blk < 3)) | (low_dev & (blk >= 3 + nblk)))
+            a = pltpu.roll(pack_in[n, 0, t].astype(F32), (LANES - HALO * g) % LANES, 1)
+            b = pltpu.roll(pack_in[n, 1, t].astype(F32), (cols + HALO - HALO * g) % LANES, 1)
+            inside = jnp.logical_not((top_dev if blk < 3 else False) | (low_dev if blk >= 3 + nblk else False))
             a_ok = inside & jnp.logical_not(first)
             b_ok = inside & jnp.logical_not(last)
             a = jnp.where(a_ok, a, 0.0)
@@ -384,29 +383,30 @@
                 y0 = mm(e, x0).reshape(step, 8, 256)
                 y1 = mm(e, x1).reshape(step, 8, 256)
                 v = jnp.concatenate([y0, y1], axis=1).astype(BF)
-                spec[step * m : step * (m + 1), pl.ds(pl.multiple_of(16 * i, 16), 16), :] = v
+                spec[step * m : step * (m + 1), 16 * i : 16 * (i + 1), :] = v
             return c
 
-        lax.fori_loop(0, next_ // 2, expand, 0)
+        for i in range(next_ // 2):
+            expand(i, 0)
 
         def columns(g, c):
-            for q in range(8):
-                b = 8 * g + q
+            for q in range(56):
+                b = 56 * g + q
                 mid[b] = mm(spec[b][:, :ku], tt[b]).astype(BF)
             return c
 
-        lax.fori_loop(0, bands // 8, columns, 0)
+        lax.fori_loop(0, bands // 56, columns, 0)
 
         def along(g, c):
-            for q in range(5):
-                t = 5 * g + q
+            for q in range(40):
+                t = 40 * g + q
                 v = jnp.concatenate([mid[t], mid[third + t], mid[2 * third + t]], axis=0)
                 v = mm(rr[t][:, : 3 * ext_r], v)
                 for k in range(3):
                     fin[third * k + t] = v[rows * k : rows * (k + 1)]
             return c
 
-        lax.fori_loop(0, third // 5, along, 0)
+        lax.fori_loop(0, third // 40, along, 0)
 
         def project(i, c):
             v = fin[:bands, pl.ds(pl.multiple_of(8 * i, 8), 8), :].reshape(bands * 8, LANES).astype(BF)
@@ -427,7 +427,7 @@
     sums = lax.fori_loop(0, nblk, products, (zero,) * 5)
     total = jnp.concatenate([jnp.sum(v, axis=0, keepdims=True) for v in sums] + [jnp.zeros((3, LANES), F32)], axis=0)
     at = 0
-    for level, (group, place, count) in enumerate(((peers, j, nbd), (peers_x, x, nx), (peers_z, z, nz))):
+    for level, (group, place, count) in enumerate(((peers, j, nbd), (peers_r, i_row, nrow))):
         red_src[level] = total
         red_in[level, place] = total
         copies = []
@@ -524,15 +524,15 @@
         vm(2, 2, 2, ck, LANES),
         vm(2, 2, 2, ck, LANES),
         vm(3, nblk, ck, LANES, dtype=F32),
-        vm(3, 8, LANES, dtype=F32),
-        vm(3, max(nbd, nx, nz), 8, LANES, dtype=F32),
+        vm(2, 8, LANES, dtype=F32),
+        vm(2, max(nbd, nx * nz), 8, LANES, dtype=F32),
         dma((4,)),
         dma((2, nbd - 1, 2)),
         dma((2, ny)),
         dma((2, ny - 1)),
         dma((2, 4)),
         dma((2, 4)),
-        dma((2, nbd + nx + nz - 3)),
+        dma((2, nbd + nx * nz - 2)),
     ]
     shape = jax.ShapeDtypeStruct((comps, rows, cols), F32)
     vmem = pl.BlockSpec(memory_space=pltpu.VMEM)

time: 137 us -> 116 us (0.85)
  Pallas kernels: 117 us -> 97.1 us
    pallas_call x1, Pallas kernels: 117 us -> 97.1 us  [local(): pl.pallas_call(functools.partial(kernel, (cols, sizes)), out_shape=(shape...]
where the time goes in v3:
time: 116 us
  Pallas kernels  97.1 us (84%)
  local copies, waits for them, and re-layouts  13.9 us (12%)
  other arithmetic  4.03 us (3%)
    pallas_call x1, Pallas kernels, local(): pl.pallas_call(functools.partial(kernel, (cols, sizes)), out_shape=(shape...  97.1 us
    unnamed x9, local copies, waits for them, and re-layouts  3.46 us

profile of v3, /device:TPU:1, one launch (start us, length us, event | category | flops | bytes accessed | tf_op | source)
XLA Modules:
  0.0 115.7 jit_solution(11435789615095746803)
XLA Ops:
  0.6 0.7 copy.33
  1.4 0.8 rev.8
  2.2 0.7 broadcast_in_dim.6
  3.0 1.3 %pad.36.basis_t = bf16[32,256]{1,0:T(8,128)(2,1)} pad(bf16[32,224]{1,0:T(8,128)(2,1)} %bitcast.13, bf16[]{:T(256)} %constant.4.clone.1), padding=0_0x0_32 | pad | bytes 30722 | tf_op jit(solution)/shard_map/jit(_pad)/pad | solution.py:495
  4.3 0.8 rev.7
  5.1 0.7 pad_maximum_fusion.1
  5.9 0.3 slice_reduce_fusion.23
  6.2 0.8 slice_reduce_fusion.24
  7.0 0.9 add_convert_fusion.1
  8.1 0.7 copy.35.basis
  8.8 0.7 select_maximum_fusion.taps
  9.5 0.8 broadcast_in_dim.8.ridge
  10.3 0.2 pad_slice_fusion.10
  11.7 0.5 add_convert_fusion
  12.2 0.2 copy.32
  12.5 0.7 pad.34.feats
  13.1 1.2 %pad.30.obs = bf16[28,32,768]{2,1,0:T(8,128)(2,1)} pad(bf16[28,32,680]{2,1,0:T(8,128)(2,1)S(1)} %copy-done, bf16[]{:T(256)} %constant.4.clone.1), padding=0_0x0_0x0_88 | pad | bytes 2594818 | tf_op jit(solution)/shard_map/jit(_pad)/pad | solution.py:491
  14.3 0.2 pad_slice_fusion.12
  14.6 0.1 stack_reshape.6
  14.7 0.1 stack_reshape.7
  14.8 1.1 pad_maximum_fusion.edges
  15.9 97.1 %shard_map.68 = (f32[32,32,85]{2,1,0:T(8,128)}, f32[32,32,85]{2,1,0:T(8,128)}) custom-call(bf16[28,32,768]{2,1,0:T(8,128)(2,1)} %pad.30.obs, bf16[2,336,768]{2,1,0:T(8,128)(2,1)} %pad_maximum_fusion.edges, bf16[4,32,256]{2,1,0:T(8,128)(2,1)} %pad.34.feats, f32[28,8,128]{2,1,0:T(8,128)} %select_maximum_fusion.taps, bf16[224,32]{1,0:T(8,128)(2,1)} %copy.35.basis, ...), custom_call_target="tpu_custom_call" | custom-call | tf_op jit(solution)/shard_map/pallas_call | solution.py:539
  113.0 1.9 %copy.38 = f32[32,32,85]{2,1,0:T(8,128)} copy(f32[32,32,85]{2,1,0:T(8,128)} %get-tuple-element.42) | data formatting | bytes 696320
  114.9 0.8 copy.39
  (22 shorter events, 1.6 us)
Async XLA Ops:
  0.6 7.4 %copy-start.2 = (bf16[224,32]{0,1:T(8,128)(2,1)S(1)}, bf16[224,32]{0,1:T(8,128)(2,1)}, u32[]{:S(2)}) copy-start(bf16[224,32]{0,1:T(8,128)(2,1)} %param.8) | copy-start | bytes 43012
  10.2 2.9 %copy-start = (bf16[28,32,680]{2,1,0:T(8,128)(2,1)S(1)}, bf16[28,32,680]{2,1,0:T(8,128)(2,1)}, u32[]{:S(2)}) copy-start(bf16[28,32,680]{2,1,0:T(8,128)(2,1)} %param.5) | copy-start | bytes 3655684
  113.0 1.9 %copy-start.1 = (f32[32,32,85]{2,1,0:T(8,128)S(1)}, f32[32,32,85]{2,1,0:T(8,128)}, u32[]{:S(2)}) copy-start(f32[32,32,85]{2,1,0:T(8,128)} %get-tuple-element.43) | copy-start | bytes 1044484

commit v4 on v3

--- a/solution.py
+++ b/solution.py
@@ -28,6 +28,11 @@
     return lax.dot_general(a, b, (((1,), (0,)), ((), ())), preferred_element_type=F32)
 
 
+def halves(v):
+    hi = v.astype(BF)
+    return hi, (v - hi.astype(F32)).astype(BF)
+
+
 def onehot(mask):
     return jnp.where(mask, 1.0, 0.0)
 
@@ -42,9 +47,9 @@
 
 
 def kernel(
-    dims, obs, edges, feats, taps, basis, basis_t, ridge,
-    out_x, out_r,
-    edge_in, line_in, lines, rows_adj, cols_adj, zed, keep, out_a, in_a, out_b, in_b,
+    dims, obs, row_taps, col_taps, basis_t, ridge_in,
+    out,
+    edges, feats, taps, ridge, raw, vpad, edge_in, line_in, lines, rows_adj, cols_adj, zed, keep, out_a, in_a, out_b, in_b,
     tt, rr, e8, p8, p8_own, spec, mid, fin, work, ext, pack, pack_in, vec, red_src, red_in,
     edge_sem, line_sem, a_sem, b_sem, row_sem, col_sem, red_sem,
 ):
@@ -55,7 +60,7 @@
     x, z = lax.axis_index("row_0"), lax.axis_index("row_1")
     j, i_row = y * nc + core, x * nz + z
     own, rows, full = obs.shape
-    bands, comps = basis.shape
+    comps, bands = basis_t.shape
     ext_r = rows + 2 * HALO
     nblk, next_ = rows // 8, ext_r // 8
     ck = comps * 8
@@ -81,6 +86,16 @@
     everyone = peers + peers_r
     for d in everyone:
         pl.semaphore_signal(barrier, inc=1, device_id=d, device_id_type=pl.DeviceIdType.MESH)
+
+    def pack_edges(g, carry):
+        sl = pl.ds(pl.multiple_of(4 * RAD * g, 16), 4 * RAD)
+        v = obs[pl.ds(4 * g, 4)].astype(F32)
+        for k, lo in enumerate((0, rows - RAD)):
+            slab = jnp.concatenate([v[q, lo : lo + RAD] for q in range(4)], axis=0)
+            edges[k, sl, :] = slab.astype(BF)
+        return carry
+
+    lax.fori_loop(0, own // 4, pack_edges, 0)
     pl.semaphore_wait(barrier, len(everyone))
 
     def remote(src, dst, send, recv, device):
@@ -93,6 +108,37 @@
     to_down = remote(edges.at[1], edge_in.at[0], edge_sem.at[1], edge_sem.at[3], down)
     to_up.start()
     to_down.start()
+
+    pad_own = feats.shape[1]
+    raw[...] = jnp.zeros_like(raw)
+    raw[:own, :TAPS] = col_taps[...]
+    raw[pad_own : pad_own + own, :TAPS] = row_taps[...]
+    t = raw[...]
+    t_hi, t_lo = halves(t)
+    gr, gp = iota((LANES, 640), 0), iota((LANES, 640), 1)
+    g1 = (gp * 5243) >> 17
+    g1, g2 = onehot(gr == g1).astype(BF), onehot(gr == gp - TAPS * g1).astype(BF)
+    prod = (mm(t_hi, g1) + mm(t_lo, g1)) * (mm(t_hi, g2) + mm(t_lo, g2))
+    p_hi, p_lo = halves(prod)
+    pp, f = iota((640, 256), 0), iota((640, 256), 1)
+    m1 = (pp * 5243) >> 17
+    m2 = pp - TAPS * m1
+    fe = f - SLOT
+    fx = (fe * 5462) >> 16
+    fy = fe - RAD * fx
+    lag = (f < 2 * TAPS - 1) & (m2 - m1 + TAPS - 1 == f)
+    edge = (fe >= 0) & (fe < RAD * RAD)
+    for k, cut in enumerate((
+        (m1 - fx == m2 - fy) & (m1 - fx > RAD) & (m1 < TAPS),
+        (m1 + fx == m2 + fy) & (m1 + fx < RAD),
+    )):
+        sel = onehot(lag | (edge & cut)).astype(BF)
+        v = (mm(p_hi, sel) + mm(p_lo, sel)).astype(BF)
+        feats[k] = v[:pad_own]
+        feats[2 + k] = v[pad_own:]
+    flip = onehot(iota((LANES, LANES), 0) + iota((LANES, LANES), 1) == TAPS - 1).astype(BF)
+    taps[:, 0:1, :] = t[:own].reshape(own, 1, LANES)
+    taps[:, 1:2, :] = mm(t_hi, flip)[pad_own : pad_own + own].reshape(own, 1, LANES)
 
     line_copies = []
     row_kind = jnp.where(low_dev, 3, 2)
@@ -144,7 +190,7 @@
     lax.fori_loop(0, own, own_cols, 0)
 
     spread = onehot(iota((comps, ck), 0) == (iota((comps, ck), 1) >> 3)).astype(BF)
-    wide = mm(basis[...], spread)
+    wide = lax.dot_general(basis_t[...], spread, (((0,), (0,)), ((), ())), preferred_element_type=F32)
     step = bands // 4
     er, el = iota((8 * step, ck), 0), iota((8 * step, ck), 1)
     for c in range(4):
@@ -152,8 +198,12 @@
         e8[8 * step * c : 8 * step * (c + 1)] = jnp.where((er & 7) == (el & 7), v, 0.0).astype(BF)
     tall = onehot(iota((ck, comps), 1) == (iota((ck, comps), 0) >> 3)).astype(BF)
     tall = mm(tall, basis_t[...]).astype(BF)
-    br, bl = iota((256, 256), 0), iota((256, 256), 1)
-    same = (br & 7) == (bl & 7)
+    br, bl = iota((bands, 256), 0), iota((bands, 256), 1)
+    same = (iota((ck, 256), 0) & 7) == (iota((ck, 256), 1) & 7)
+    kr, kl = iota((ck, comps), 0), iota((ck, comps), 1)
+    ridge_col = jnp.sum(jnp.where(kl == (kr >> 3), ridge_in[...], 0.0), axis=1, keepdims=True)
+    ridge[...] = jnp.broadcast_to(ridge_col, (ck, LANES))
+    vpad[...] = jnp.zeros_like(vpad)
 
     def widen(start):
         return jnp.where(same, mm(tall, onehot(br == start + (bl >> 3)).astype(BF)), 0.0).astype(BF)
@@ -251,10 +301,12 @@
         above = jnp.where(above_ok, above, jnp.zeros_like(above))
         below = jnp.where(below_ok, below, jnp.zeros_like(below))
         v = mm(rows_adj[g][:, : 4 * rows + 8 * RAD], jnp.concatenate([mine, above, below], axis=0))
+        vpad[:, :full] = v
+        v = vpad[...]
         wins = []
         for k in range(ny):
             start = nc * cols * k - RAD
-            wins.append(pltpu.roll(v, (full - start) % full, 1)[:, :256].astype(BF))
+            wins.append(pltpu.roll(v, (v.shape[1] - start) % v.shape[1], 1)[:, :256].astype(BF))
         for q in range(4):
             u = jnp.concatenate([t[rows * q : rows * (q + 1)] for t in wins], axis=0)
             u = mm(u[:, :kw], cols_adj[4 * g + q])
@@ -454,25 +506,11 @@
         xs = alpha * a + alpha2 * (gain * a - alpha * b)
         rs = (a - alpha * b) - alpha2 * (gain * b - alpha * c)
         sl = pl.ds(pl.multiple_of(8 * i, 8), 8)
-        out_x[:, sl, :] = xs.reshape(comps, 8, LANES)[:, :, :cols]
-        out_r[:, sl, :] = rs.reshape(comps, 8, LANES)[:, :, :cols]
+        out[0, :, sl, :] = xs.reshape(comps, 8, LANES)
+        out[1, :, sl, :] = rs.reshape(comps, 8, LANES)
         return carry
 
     lax.fori_loop(0, nblk, finish, 0)
-
-
-def features(t):
-    wide = jnp.pad(t, ((0, 0), (0, 0), (TAPS - 1, TAPS - 1)))
-    auto = sum(t[:, :, m : m + 1] * wide[:, :, m : m + 2 * TAPS - 1] for m in range(TAPS))
-    tail = jnp.pad(t[:, :, RAD + 1 :], ((0, 0), (0, 0), (0, RAD)))
-    cut = 0.0
-    for m in range(RAD):
-        v = tail[:, :, m : m + RAD]
-        cut = cut + v[:, :, :, None] * v[:, :, None, :]
-    cut = cut.reshape(t.shape[0], t.shape[1], RAD * RAD)
-    auto = jnp.pad(auto, ((0, 0), (0, 0), (0, SLOT - 2 * TAPS + 1)))
-    both = jnp.concatenate([auto, cut], axis=2)
-    return jnp.pad(both, ((0, 0), (0, -t.shape[1] % 16), (0, 256 - both.shape[2]))).astype(BF)
 
 
 def local(height, width, sizes, observed, row_taps, col_taps, spectral_basis, ridge_weights):
@@ -488,20 +526,21 @@
     ku = -(-(cols + 2 * HALO) // 16) * 16
     kw = -(-(nc * cols + 2 * RAD) // 16) * 16
 
-    obs = jnp.pad(observed, ((0, 0), (0, 0), (0, full - width)))
-    edges = jnp.stack([obs[:, :RAD].reshape(own * RAD, full), obs[:, rows - RAD :].reshape(own * RAD, full)])
-    feats = features(jnp.stack([col_taps, col_taps[:, ::-1], row_taps, row_taps[:, ::-1]]))
-    taps = jnp.pad(jnp.stack([col_taps, row_taps[:, ::-1]], axis=1), ((0, 0), (0, 6), (0, LANES - TAPS)))
-    basis_t = jnp.pad(spectral_basis.T, ((0, 0), (0, 256 - bands)))
-    ridge = jnp.broadcast_to(jnp.repeat(ridge_weights, 8)[:, None], (ck, LANES))
+    pad_own = -(-own // 16) * 16
 
     def vm(*shape, dtype=BF):
         return pltpu.VMEM(shape, dtype)
 
     dma = pltpu.SemaphoreType.DMA
     scratch = [
-        vm(2, own * RAD, full),
-        vm(nbd, 2, feats.shape[1], 256),
+        vm(2, own * RAD, width),
+        vm(4, pad_own, 256),
+        vm(own, 8, LANES, dtype=F32),
+        vm(ck, LANES, dtype=F32),
+        vm(2 * pad_own, LANES, dtype=F32),
+        vm(4 * rows, full, dtype=F32),
+        vm(2, own * RAD, width),
+        vm(nbd, 2, pad_own, 256),
         vm(2, bands, 256, dtype=F32),
         vm(own // 4, 4 * rows, 256),
         vm(own, kw, 256),
@@ -534,18 +573,18 @@
         dma((2, 4)),
         dma((2, nbd + nx * nz - 2)),
     ]
-    shape = jax.ShapeDtypeStruct((comps, rows, cols), F32)
     vmem = pl.BlockSpec(memory_space=pltpu.VMEM)
-    return pl.pallas_call(
+    both = pl.pallas_call(
         functools.partial(kernel, (cols, sizes)),
-        out_shape=(shape, shape),
-        in_specs=[vmem] * 7,
-        out_specs=(vmem, vmem),
+        out_shape=jax.ShapeDtypeStruct((2, comps, rows, LANES), F32),
+        in_specs=[vmem] * 5,
+        out_specs=vmem,
         scratch_shapes=scratch,
         compiler_params=pltpu.CompilerParams(
             collective_id=0, has_side_effects=True, vmem_limit_bytes=67043328
         ),
-    )(obs, edges, feats, taps, spectral_basis, basis_t, ridge)
+    )(observed, row_taps, col_taps, spectral_basis.T, ridge_weights[None, :])
+    return both[0, :, :, :cols], both[1, :, :, :cols]
 
 
 def solution(mesh):

time: 116 us -> 100 us (0.86)
  local copies, waits for them, and re-layouts: 13.9 us -> 2.24 us
  other arithmetic: 4.03 us -> 0 us
    another operation x5 -> x0, other arithmetic: 3.93 us -> none  [the longest x2 1.42 us: whole(): jax.shard_map(functools.partial(local, height, width, sizes), mesh=split,...]
    unnamed x9 -> x0, local copies, waits for them, and re-layouts: 3.46 us -> none
    pad x3 -> x0, local copies, waits for them, and re-layouts: 3.21 us -> none  [the longest x1 1.33 us: local(): basis_t = jnp.pad(spectral_basis.T, ((0, 0), (0, 256 - bands)))]
    slice x17 -> x0, local copies, waits for them, and re-layouts: 2.91 us -> none  [the longest x12 1.41 us: features(): v = tail[:, :, m:m + RAD]]
    squeeze x0 -> x1, local copies, waits for them, and re-layouts: none -> 2.24 us  [local(): return (both[0, :, :, :cols], both[1, :, :, :cols])]
    rev x2 -> x0, local copies, waits for them, and re-layouts: 1.58 us -> none  [the longest x1 0.79 us: local(): row_taps[:, ::-1]]
    broadcast_in_dim x3 -> x0, local copies, waits for them, and re-layouts: 1.57 us -> none  [local(): ridge = jnp.broadcast_to(jnp.repeat(ridge_weights, 8)[:, None], (ck, LANES))]
where the time goes in v4:
time: 100 us; the launch traced here: 99.8 us
  Pallas kernels  97 us (97%)
  local copies, waits for them, and re-layouts  2.24 us (2%)
    pallas_call x1, Pallas kernels, local(): pl.pallas_call(functools.partial(kernel, (cols, sizes)), out_shape=jax.Sh...  97 us
    squeeze x1, local copies, waits for them, and re-layouts, local(): return (both[0, :, :, :cols], both[1, :, :, :cols])  2.24 us

profile of v4, /device:TPU:1, one launch (start us, length us, event | category | flops | bytes accessed | tf_op | source)
XLA Modules:
  0.0 99.8 jit_solution(12113097656059652363)
XLA Ops:
  0.6 97.0 %shard_map.68 = f32[2,32,32,128]{3,2,1,0:T(8,128)} custom-call(bf16[28,32,680]{2,1,0:T(8,128)(2,1)} %obs.1, f32[28,25]{1,0:T(8,128)} %row_taps.1, f32[28,25]{1,0:T(8,128)} %col_taps.1, bf16[32,224]{1,0:T(8,128)(2,1)} %bitcast.6, f32[1,32]{1,0:T(1,128)} %bitcast.7), custom_call_target="tpu_custom_call" | custom-call | tf_op jit(solution)/shard_map/pallas_call | solution.py:577
  97.6 2.2 %slice_bitcast_fusion = (f32[32,32,85]{2,1,0:T(8,128)}, f32[32,32,85]{2,1,0:T(8,128)}) fusion(f32[2,32,32,128]{3,2,1,0:T(8,128)} %shard_map.68), kind=kLoop, calls=%fused_computation | loop fusion | bytes 1392640 | tf_op jit(solution)/shard_map/squeeze | solution.py:587

commit v5 on v4

--- a/solution.py
+++ b/solution.py
@@ -62,7 +62,7 @@
     own, rows, full = obs.shape
     comps, bands = basis_t.shape
     ext_r = rows + 2 * HALO
-    nblk, next_ = rows // 8, ext_r // 8
+    nblk = rows // 8
     ck = comps * 8
     ku = tt.shape[1]
     first, last = j == 0, j == nbd - 1
@@ -258,12 +258,16 @@
     lane16 = iota((16, LANES), 1)
 
     def rr_pair(p, carry):
+        def row_of(n):
+            b = n & 127
+            return jnp.where(b < rows, b + HALO, jnp.where(b < rows + HALO, b - rows, b))
+
         def hit(n):
-            a, b = 16 * p + (n >> 7), n & 127
+            a, b = 16 * p + (n >> 7), row_of(n)
             return jnp.where((b < ext_r) & (b >= a) & (b - a <= 2 * HALO), b - a, -1)
 
         def edge_hit(n):
-            a, b = 16 * p + (n >> 7), (n & 127) - HALO
+            a, b = 16 * p + (n >> 7), row_of(n) - HALO
             a, b = jnp.where(low_dev, rows - 1 - a, a), jnp.where(low_dev, rows - 1 - b, b)
             ok = (top_dev | low_dev) & (a >= 0) & (a < RAD) & (b >= 0) & (b < RAD)
             return jnp.where(ok, SLOT + RAD * a + b, -1)
@@ -374,80 +378,98 @@
         lax.fori_loop(0, nblk, collect, 0)
 
     chunk = ck // 4
-    per = next_ // 2
     lane_c = iota((chunk, LANES), 1)
     lane_k = iota((ck, LANES), 1)
 
     def normal(n, carry):
         def stage(i, c):
-            ext[n, 3 + i] = vec[n, i].astype(BF)
+            ext[n, i] = vec[n, i].astype(BF)
             return c
 
         lax.fori_loop(0, nblk, stage, 0)
-        r_up = remote(ext.at[n, pl.ds(3, 3)], ext.at[n, pl.ds(3 + nblk, 3)], row_sem.at[n, 0], row_sem.at[n, 2], up)
-        r_down = remote(ext.at[n, pl.ds(nblk, 3)], ext.at[n, pl.ds(0, 3)], row_sem.at[n, 1], row_sem.at[n, 3], down)
+        r_up = remote(ext.at[n, pl.ds(0, 3)], ext.at[n, pl.ds(nblk + 3, 3)], row_sem.at[n, 0], row_sem.at[n, 2], up)
+        r_down = remote(ext.at[n, pl.ds(nblk - 3, 3)], ext.at[n, pl.ds(nblk, 3)], row_sem.at[n, 1], row_sem.at[n, 3], down)
         r_up.start()
         r_down.start()
-        r_up.wait()
-        r_down.wait()
-
-        def packing(c, cc):
-            t, part = c // 4, lax.rem(c, 4)
-            sl = pl.ds(pl.multiple_of(chunk * part, chunk), chunk)
-            a = jnp.zeros((chunk, LANES), F32)
-            b = a
-            for g in range(per):
-                v = ext[n, per * t + g, sl, :].astype(F32)
-                m = (lane_c >= HALO * g) & (lane_c < HALO * (g + 1))
-                a = jnp.where(m, pltpu.roll(v, HALO * g, 1) if g else v, a)
-                b = jnp.where(m, pltpu.roll(v, (HALO * g - cols + HALO) % LANES, 1), b)
-            pack[n, 0, t, sl, :] = a.astype(BF)
-            pack[n, 1, t, sl, :] = b.astype(BF)
-            return cc
-
-        lax.fori_loop(0, 8, packing, 0)
-        c_left = remote(pack.at[n, 0], pack_in.at[n, 1], col_sem.at[n, 0], col_sem.at[n, 2], left)
-        c_right = remote(pack.at[n, 1], pack_in.at[n, 0], col_sem.at[n, 1], col_sem.at[n, 3], right)
-        c_left.start()
-        c_right.start()
-        c_left.wait()
-        c_right.wait()
-
-        def block(blk):
-            t, g = blk // per, blk % per
+
+        def packing(t, blocks):
+            def part(c, cc):
+                sl = pl.ds(pl.multiple_of(chunk * c, chunk), chunk)
+                a = jnp.zeros((chunk, LANES), F32)
+                b = a
+                for g, blk in enumerate(blocks):
+                    v = ext[n, blk, sl, :].astype(F32)
+                    m = (lane_c >= HALO * g) & (lane_c < HALO * (g + 1))
+                    a = jnp.where(m, pltpu.roll(v, HALO * g, 1) if g else v, a)
+                    b = jnp.where(m, pltpu.roll(v, (HALO * g - cols + HALO) % LANES, 1), b)
+                pack[n, 0, t, sl, :] = a.astype(BF)
+                pack[n, 1, t, sl, :] = b.astype(BF)
+                return cc
+
+            lax.fori_loop(0, ck // chunk, part, 0)
+
+        def swap(first_t, count, k):
+            sl = pl.ds(first_t, count)
+            a = remote(pack.at[n, 0, sl], pack_in.at[n, 1, sl], col_sem.at[n, k], col_sem.at[n, k + 2], left)
+            b = remote(pack.at[n, 1, sl], pack_in.at[n, 0, sl], col_sem.at[n, k + 1], col_sem.at[n, k + 3], right)
+            a.start()
+            b.start()
+            return a, b
+
+        def block(blk, t, g):
             mine = pltpu.roll(ext[n, blk].astype(F32), HALO, 1)
             a = pltpu.roll(pack_in[n, 0, t].astype(F32), (LANES - HALO * g) % LANES, 1)
             b = pltpu.roll(pack_in[n, 1, t].astype(F32), (cols + HALO - HALO * g) % LANES, 1)
-            inside = jnp.logical_not((top_dev if blk < 3 else False) | (low_dev if blk >= 3 + nblk else False))
-            a_ok = inside & jnp.logical_not(first)
-            b_ok = inside & jnp.logical_not(last)
+            a_ok, b_ok = jnp.logical_not(first), jnp.logical_not(last)
+            if blk >= nblk:
+                inside = jnp.logical_not(top_dev if blk < nblk + 3 else low_dev)
+                a_ok, b_ok = a_ok & inside, b_ok & inside
+                mine = jnp.where(inside, mine, 0.0)
             a = jnp.where(a_ok, a, 0.0)
             b = jnp.where(b_ok, b, 0.0)
-            mine = jnp.where(inside, mine, 0.0)
             t0 = jnp.where(lane_k < HALO, a, jnp.where(lane_k < HALO + cols, mine, b))
             t1 = jnp.where(lane_k < cols + 2 * HALO - LANES, b, 0.0)
             return jnp.concatenate([t0, t1], axis=1).astype(BF)
 
-        def expand(i, c):
-            x0, x1 = block(2 * i), block(2 * i + 1)
+        def expand(row, x0, x1):
             for m in range(4):
                 e = e8[8 * step * m : 8 * step * (m + 1)]
                 y0 = mm(e, x0).reshape(step, 8, 256)
                 y1 = mm(e, x1).reshape(step, 8, 256)
                 v = jnp.concatenate([y0, y1], axis=1).astype(BF)
-                spec[step * m : step * (m + 1), 16 * i : 16 * (i + 1), :] = v
-            return c
-
-        for i in range(next_ // 2):
-            expand(i, 0)
-
-        def columns(g, c):
-            for q in range(56):
-                b = 56 * g + q
-                mid[b] = mm(spec[b][:, :ku], tt[b]).astype(BF)
-            return c
-
-        lax.fori_loop(0, bands // 56, columns, 0)
+                spec[step * m : step * (m + 1), row : row + 16, :] = v
+
+        def columns(lo, count):
+            def body(g, c):
+                for q in range(56):
+                    b = 56 * g + q
+                    mid[b, lo : lo + count] = mm(spec[b, lo : lo + count][:, :ku], tt[b]).astype(BF)
+                return c
+
+            lax.fori_loop(0, bands // 56, body, 0)
+
+        packing(0, range(nblk))
+        own_edges = swap(0, 1, 0)
+        for c in own_edges:
+            c.wait()
+        for i in range(nblk // 2):
+            expand(16 * i, block(2 * i, 0, 2 * i), block(2 * i + 1, 0, 2 * i + 1))
+        r_up.wait()
+        r_down.wait()
+        packing(1, range(nblk, nblk + 3))
+        packing(2, range(nblk + 3, nblk + 6))
+        halo_edges = swap(1, 2, 4)
+        columns(0, rows)
+        for c in halo_edges:
+            c.wait()
+        for i in range(3):
+            k0, k1 = 2 * i, 2 * i + 1
+            expand(
+                rows + 16 * i,
+                block(nblk + k0, 1 + k0 // 3, k0 % 3),
+                block(nblk + k1, 1 + k1 // 3, k1 % 3),
+            )
+        columns(rows, ext_r - rows)
 
         def along(g, c):
             for q in range(40):
@@ -560,8 +582,8 @@
         vm(3 * third, rows, LANES, dtype=F32),
         vm(bands // 8, LANES, LANES, dtype=F32),
         vm(2, ext_r // 8, ck, LANES),
-        vm(2, 2, 2, ck, LANES),
-        vm(2, 2, 2, ck, LANES),
+        vm(2, 2, 3, ck, LANES),
+        vm(2, 2, 3, ck, LANES),
         vm(3, nblk, ck, LANES, dtype=F32),
         vm(2, 8, LANES, dtype=F32),
         vm(2, max(nbd, nx * nz), 8, LANES, dtype=F32),
@@ -570,7 +592,7 @@
         dma((2, ny)),
         dma((2, ny - 1)),
         dma((2, 4)),
-        dma((2, 4)),
+        dma((2, 8)),
         dma((2, nbd + nx * nz - 2)),
     ]
     vmem = pl.BlockSpec(memory_space=pltpu.VMEM)

time: 100 us -> 97.2 us (0.972)
  Pallas kernels: 97 us -> 94.2 us
    pallas_call x1, Pallas kernels: 97 us -> 94.2 us  [local(): pl.pallas_call(functools.partial(kernel, (cols, sizes)), out_shape=jax.Sh...]
where the time goes in v5:
time: 97.2 us; the launch traced here: 97.1 us
  Pallas kernels  94.2 us (97%)
  local copies, waits for them, and re-layouts  2.24 us (2%)
    pallas_call x1, Pallas kernels, local(): pl.pallas_call(functools.partial(kernel, (cols, sizes)), out_shape=jax.Sh...  94.2 us
    squeeze x1, local copies, waits for them, and re-layouts, local(): return (both[0, :, :, :cols], both[1, :, :, :cols])  2.24 us

profile of v5, /device:TPU:1, one launch (start us, length us, event | category | flops | bytes accessed | tf_op | source)
XLA Modules:
  0.0 97.1 jit_solution(14197268515838963071)
XLA Ops:
  0.6 94.2 %shard_map.68 = f32[2,32,32,128]{3,2,1,0:T(8,128)} custom-call(bf16[28,32,680]{2,1,0:T(8,128)(2,1)} %obs.1, f32[28,25]{1,0:T(8,128)} %row_taps.1, f32[28,25]{1,0:T(8,128)} %col_taps.1, bf16[32,224]{1,0:T(8,128)(2,1)} %bitcast.6, f32[1,32]{1,0:T(1,128)} %bitcast.7), custom_call_target="tpu_custom_call" | custom-call | tf_op jit(solution)/shard_map/pallas_call | solution.py:599
  94.8 2.2 %slice_bitcast_fusion = (f32[32,32,85]{2,1,0:T(8,128)}, f32[32,32,85]{2,1,0:T(8,128)}) fusion(f32[2,32,32,128]{3,2,1,0:T(8,128)} %shard_map.68), kind=kLoop, calls=%fused_computation | loop fusion | bytes 1392640 | tf_op jit(solution)/shard_map/squeeze | solution.py:609

commit v6 on v5

--- a/solution.py
+++ b/solution.py
@@ -50,7 +50,7 @@
     dims, obs, row_taps, col_taps, basis_t, ridge_in,
     out,
     edges, feats, taps, ridge, raw, vpad, edge_in, line_in, lines, rows_adj, cols_adj, zed, keep, out_a, in_a, out_b, in_b,
-    tt, rr, e8, p8, p8_own, spec, mid, fin, work, ext, pack, pack_in, vec, red_src, red_in,
+    tt, rr, e8, p8, p8_own, spec, mid, fin, work, ext, pack, pack_in, vec, red_src, red_in, tight, tight_in,
     edge_sem, line_sem, a_sem, b_sem, row_sem, col_sem, red_sem,
 ):
     cols, sizes = dims
@@ -82,8 +82,15 @@
     peers = [at_band(lax.rem(j + s, nbd)) for s in range(1, nbd)]
     peers_r = [at_row(lax.rem(i_row + s, nrow)) for s in range(1, nrow)]
 
+
+    def corner(di, dj):
+        ii, jj = lax.rem(i_row + nrow + di, nrow), lax.rem(j + nbd + dj, nbd)
+        return (jj // nc, lax.rem(jj, nc), ii // nz, lax.rem(ii, nz))
+
+    corners = {(di, dj): corner(di, dj) for di in (-1, 1) for dj in (-1, 1)}
+
     barrier = pltpu.get_barrier_semaphore()
-    everyone = peers + peers_r
+    everyone = peers + peers_r + list(corners.values())
     for d in everyone:
         pl.semaphore_signal(barrier, inc=1, device_id=d, device_id_type=pl.DeviceIdType.MESH)
 
@@ -345,15 +352,12 @@
     for idx, off in enumerate(offsets):
         k = lax.rem(y + off, ny)
 
-        def project(i, carry):
-            v = zed[k, :, pl.ds(pl.multiple_of(8 * i, 8), 8), :].reshape(own * 8, 256).astype(BF)
+        for i in range(nblk):
+            v = zed[k, :, 8 * i : 8 * (i + 1), :].reshape(own * 8, 256).astype(BF)
             v = mm(p8_own[:, : own * 8], v)
             lo, hi = v[:, :LANES], v[:, LANES:]
             keep[idx, i] = jnp.where(core == 0, lo, hi)
             out_a[idx, i] = jnp.where(core == 0, hi, lo).astype(BF)
-            return carry
-
-        lax.fori_loop(0, nblk, project, 0)
         c = remote(out_a.at[idx], in_a.at[idx], a_sem.at[0, idx], a_sem.at[1, idx], partner)
         c.start()
         a_copies.append(c)
@@ -387,10 +391,15 @@
             return c
 
         lax.fori_loop(0, nblk, stage, 0)
-        r_up = remote(ext.at[n, pl.ds(0, 3)], ext.at[n, pl.ds(nblk + 3, 3)], row_sem.at[n, 0], row_sem.at[n, 2], up)
-        r_down = remote(ext.at[n, pl.ds(nblk - 3, 3)], ext.at[n, pl.ds(nblk, 3)], row_sem.at[n, 1], row_sem.at[n, 3], down)
-        r_up.start()
-        r_down.start()
+        cut = LANES - cols
+        for k, lo in enumerate((0, nblk - 3)):
+            a, b, c = (vec[n, lo + q] for q in range(3))
+            b = pltpu.roll(b, cols, 1)
+            c = pltpu.roll(c, cols - cut, 1)
+            tight[n, k, 0] = jnp.where(lane_k < cols, a, b).astype(BF)
+            tight[n, k, 1] = jnp.where(lane_k < cols - cut, b, c).astype(BF)
+        r_up = remote(tight.at[n, 0], tight_in.at[n, 1], row_sem.at[n, 0], row_sem.at[n, 2], up)
+        r_down = remote(tight.at[n, 1], tight_in.at[n, 0], row_sem.at[n, 1], row_sem.at[n, 3], down)
 
         def packing(t, blocks):
             def part(c, cc):
@@ -408,13 +417,10 @@
 
             lax.fori_loop(0, ck // chunk, part, 0)
 
-        def swap(first_t, count, k):
-            sl = pl.ds(first_t, count)
-            a = remote(pack.at[n, 0, sl], pack_in.at[n, 1, sl], col_sem.at[n, k], col_sem.at[n, k + 2], left)
-            b = remote(pack.at[n, 1, sl], pack_in.at[n, 0, sl], col_sem.at[n, k + 1], col_sem.at[n, k + 3], right)
-            a.start()
-            b.start()
-            return a, b
+        def to(src, dst, k, device):
+            c = remote(pack.at[(n,) + src], pack_in.at[(n,) + dst], col_sem.at[n, 0, k], col_sem.at[n, 1, k], device)
+            c.start()
+            return c
 
         def block(blk, t, g):
             mine = pltpu.roll(ext[n, blk].astype(F32), HALO, 1)
@@ -449,17 +455,30 @@
             lax.fori_loop(0, bands // 56, body, 0)
 
         packing(0, range(nblk))
-        own_edges = swap(0, 1, 0)
+        own_edges = [to((0, 0), (1, 0), 0, left), to((1, 0), (0, 0), 1, right)]
+        r_up.start()
+        r_down.start()
+        packing(1, range(nblk - 3, nblk))
+        packing(2, range(3))
+        halo_edges = [
+            to((1, 1), (0, 1), 2, corners[1, 1]),
+            to((0, 1), (1, 1), 3, corners[1, -1]),
+            to((1, 2), (0, 2), 4, corners[-1, 1]),
+            to((0, 2), (1, 2), 5, corners[-1, -1]),
+        ]
         for c in own_edges:
             c.wait()
         for i in range(nblk // 2):
             expand(16 * i, block(2 * i, 0, 2 * i), block(2 * i + 1, 0, 2 * i + 1))
+        columns(0, rows)
         r_up.wait()
         r_down.wait()
-        packing(1, range(nblk, nblk + 3))
-        packing(2, range(nblk + 3, nblk + 6))
-        halo_edges = swap(1, 2, 4)
-        columns(0, rows)
+        for k in range(2):
+            a, b = tight_in[n, k, 0].astype(F32), tight_in[n, k, 1].astype(F32)
+            ext[n, nblk + 3 * k] = tight_in[n, k, 0]
+            b1 = jnp.where(lane_k < cut, pltpu.roll(a, cut, 1), pltpu.roll(b, cut, 1))
+            ext[n, nblk + 3 * k + 1] = b1.astype(BF)
+            ext[n, nblk + 3 * k + 2] = pltpu.roll(b, 2 * cut, 1).astype(BF)
         for c in halo_edges:
             c.wait()
         for i in range(3):
@@ -482,12 +501,9 @@
 
         lax.fori_loop(0, third // 40, along, 0)
 
-        def project(i, c):
-            v = fin[:bands, pl.ds(pl.multiple_of(8 * i, 8), 8), :].reshape(bands * 8, LANES).astype(BF)
+        for i in range(nblk):
+            v = fin[:bands, 8 * i : 8 * (i + 1), :].reshape(bands * 8, LANES).astype(BF)
             vec[n + 1, i] = mm(p8[...], v) + ridge[...] * vec[n, i]
-            return c
-
-        lax.fori_loop(0, nblk, project, 0)
         return carry
 
     lax.fori_loop(0, 2, normal, 0)
@@ -587,12 +603,14 @@
         vm(3, nblk, ck, LANES, dtype=F32),
         vm(2, 8, LANES, dtype=F32),
         vm(2, max(nbd, nx * nz), 8, LANES, dtype=F32),
+        vm(2, 2, 2, ck, LANES),
+        vm(2, 2, 2, ck, LANES),
         dma((4,)),
         dma((2, nbd - 1, 2)),
         dma((2, ny)),
         dma((2, ny - 1)),
         dma((2, 4)),
-        dma((2, 8)),
+        dma((2, 2, 6)),
         dma((2, nbd + nx * nz - 2)),
     ]
     vmem = pl.BlockSpec(memory_space=pltpu.VMEM)

time: 97.2 us -> 92 us (0.947)
  Pallas kernels: 94.2 us -> 89 us
    pallas_call x1, Pallas kernels: 94.2 us -> 89 us  [local(): pl.pallas_call(functools.partial(kernel, (cols, sizes)), out_shape=jax.Sh...]
where the time goes in v6:
time: 92 us; the launch traced here: 91.8 us
  Pallas kernels  89 us (97%)
  local copies, waits for them, and re-layouts  2.24 us (2%)
    pallas_call x1, Pallas kernels, local(): pl.pallas_call(functools.partial(kernel, (cols, sizes)), out_shape=jax.Sh...  89 us
    squeeze x1, local copies, waits for them, and re-layouts, local(): return (both[0, :, :, :cols], both[1, :, :, :cols])  2.24 us

profile of v6, /device:TPU:1, one launch (start us, length us, event | category | flops | bytes accessed | tf_op | source)
XLA Modules:
  0.0 91.8 jit_solution(8174188070546970139)
XLA Ops:
  0.6 89.0 %shard_map.68 = f32[2,32,32,128]{3,2,1,0:T(8,128)} custom-call(bf16[28,32,680]{2,1,0:T(8,128)(2,1)} %obs.1, f32[28,25]{1,0:T(8,128)} %row_taps.1, f32[28,25]{1,0:T(8,128)} %col_taps.1, bf16[32,224]{1,0:T(8,128)(2,1)} %bitcast.6, f32[1,32]{1,0:T(1,128)} %bitcast.7), custom_call_target="tpu_custom_call" | custom-call | tf_op jit(solution)/shard_map/pallas_call | solution.py:617
  89.6 2.2 %slice_bitcast_fusion = (f32[32,32,85]{2,1,0:T(8,128)}, f32[32,32,85]{2,1,0:T(8,128)}) fusion(f32[2,32,32,128]{3,2,1,0:T(8,128)} %shard_map.68), kind=kLoop, calls=%fused_computation | loop fusion | bytes 1392640 | tf_op jit(solution)/shard_map/squeeze | solution.py:627

commit v7 on v6

--- a/solution.py
+++ b/solution.py
@@ -111,10 +111,14 @@
             device_id=device, device_id_type=pl.DeviceIdType.MESH,
         )
 
-    to_up = remote(edges.at[0], edge_in.at[1], edge_sem.at[0], edge_sem.at[2], up)
-    to_down = remote(edges.at[1], edge_in.at[0], edge_sem.at[1], edge_sem.at[3], down)
-    to_up.start()
-    to_down.start()
+    early = (own // 4 + 1) // 2
+    edge_copies = []
+    for part, sl in enumerate((pl.ds(0, 4 * RAD * early), pl.ds(4 * RAD * early, RAD * own - 4 * RAD * early))):
+        a = remote(edges.at[0, sl], edge_in.at[1, sl], edge_sem.at[0, part, 0], edge_sem.at[1, part, 0], up)
+        b = remote(edges.at[1, sl], edge_in.at[0, sl], edge_sem.at[0, part, 1], edge_sem.at[1, part, 1], down)
+        a.start()
+        b.start()
+        edge_copies.append((a, b))
 
     pad_own = feats.shape[1]
     raw[...] = jnp.zeros_like(raw)
@@ -228,7 +232,7 @@
     wide_n = 16 * LANES
 
     def shifted(depth, hit, edge_hit):
-        f, n = iota((depth, wide_n), 0), iota((depth, wide_n), 1)
+        f, n = iota((depth, wide_n), 0), iota((1, wide_n), 1)
         s = onehot(f == hit(n))
         if edge_hit is not None:
             s = s - onehot(f == edge_hit(n))
@@ -300,20 +304,18 @@
 
     lax.fori_loop(0, rows // 16, rr_pair, 0)
 
-    to_up.wait()
-    to_down.wait()
     above_ok, below_ok = i_row > 0, i_row < nrow - 1
 
-    def adjoint(g, carry):
-        e = pl.ds(pl.multiple_of(4 * RAD * g, 16), 4 * RAD)
+    def adjoint(g):
+        e = slice(4 * RAD * g, 4 * RAD * (g + 1))
         above = edge_in[0, e]
         below = edge_in[1, e]
-        mine = obs[pl.ds(4 * g, 4)].reshape(4 * rows, full)
+        mine = obs[4 * g : 4 * g + 4].reshape(4 * rows, full)
         above = jnp.where(above_ok, above, jnp.zeros_like(above))
         below = jnp.where(below_ok, below, jnp.zeros_like(below))
         v = mm(rows_adj[g][:, : 4 * rows + 8 * RAD], jnp.concatenate([mine, above, below], axis=0))
-        vpad[:, :full] = v
-        v = vpad[...]
+        vpad[g % 2, :, :full] = v
+        v = vpad[g % 2]
         wins = []
         for k in range(ny):
             start = nc * cols * k - RAD
@@ -323,10 +325,15 @@
             u = mm(u[:, :kw], cols_adj[4 * g + q])
             for k in range(ny):
                 zed[k, 4 * g + q] = u[rows * k : rows * (k + 1)]
-        return carry
-
-    lax.fori_loop(0, own // 4, adjoint, 0)
-
+
+    for g in range(own // 4):
+        if g in (0, early):
+            for c in edge_copies[g // max(early, 1)]:
+                c.wait()
+        adjoint(g)
+
+    lane_k = iota((ck, LANES), 1)
+    cut = LANES - cols
     offsets = [s for s in (2, 1, 3, 0) if s < ny]
     a_copies, b_copies = [], []
 
@@ -334,15 +341,17 @@
         a_copies[idx].wait()
         done = idx == len(offsets) - 1
 
-        def add(i, carry):
-            v = keep[idx, i] + in_a[idx, i].astype(F32)
-            if done:
-                vec[0, i] = v
-            else:
-                out_b[idx, i] = v.astype(BF)
-            return carry
-
-        lax.fori_loop(0, nblk, add, 0)
+        def add(i):
+            return keep[idx, i] + in_a[idx, i].astype(F32)
+
+        if done:
+            for i in range(nblk):
+                vec[0, i] = add(i)
+        else:
+            b = pltpu.roll(add(1), cols, 1)
+            out_b[idx, 0] = jnp.where(lane_k < cols, add(0), b).astype(BF)
+            out_b[idx, 1] = jnp.where(lane_k < cols - cut, b, pltpu.roll(add(2), cols - cut, 1)).astype(BF)
+            out_b[idx, 2] = add(3).astype(BF)
         if not done:
             dest = (lax.rem(y + offsets[idx], ny), core, x, z)
             c = remote(out_b.at[idx], in_b.at[idx], b_sem.at[0, idx], b_sem.at[1, idx], dest)
@@ -372,18 +381,15 @@
         lax.fori_loop(p0, p0 + 2, functools.partial(tt_pair, depth=256), 0)
 
     mid[pl.ds(bands, mid.shape[0] - bands)] = jnp.zeros((mid.shape[0] - bands, ext_r, LANES), BF)
-    for idx, c in enumerate(b_copies):
+    for c in b_copies:
         c.wait()
-
-        def collect(i, carry):
-            vec[0, i] = vec[0, i] + in_b[idx, i].astype(F32)
-            return carry
-
-        lax.fori_loop(0, nblk, collect, 0)
+    a, b, c = (sum(in_b[idx, t].astype(F32) for idx in range(ny - 1)) for t in range(3))
+    b1 = jnp.where(lane_k < cut, pltpu.roll(a, cut, 1), pltpu.roll(b, cut, 1))
+    for i, v in enumerate((a, b1, pltpu.roll(b, 2 * cut, 1), c)):
+        vec[0, i] = vec[0, i] + jnp.where(lane_k < cols, v, 0.0)
 
     chunk = ck // 4
     lane_c = iota((chunk, LANES), 1)
-    lane_k = iota((ck, LANES), 1)
 
     def normal(n, carry):
         def stage(i, c):
@@ -391,7 +397,6 @@
             return c
 
         lax.fori_loop(0, nblk, stage, 0)
-        cut = LANES - cols
         for k, lo in enumerate((0, nblk - 3)):
             a, b, c = (vec[n, lo + q] for q in range(3))
             b = pltpu.roll(b, cols, 1)
@@ -576,7 +581,7 @@
         vm(own, 8, LANES, dtype=F32),
         vm(ck, LANES, dtype=F32),
         vm(2 * pad_own, LANES, dtype=F32),
-        vm(4 * rows, full, dtype=F32),
+        vm(2, 4 * rows, full, dtype=F32),
         vm(2, own * RAD, width),
         vm(nbd, 2, pad_own, 256),
         vm(2, bands, 256, dtype=F32),
@@ -586,8 +591,8 @@
         vm(ny, nblk, ck, LANES, dtype=F32),
         vm(ny, nblk, ck, LANES),
         vm(ny, nblk, ck, LANES),
-        vm(ny - 1, nblk, ck, LANES),
-        vm(ny - 1, nblk, ck, LANES),
+        vm(ny - 1, 3, ck, LANES),
+        vm(ny - 1, 3, ck, LANES),
         vm(bands, ku, LANES),
         vm(third, 3 * rows, 256),
         vm(bands * 8, ck),
@@ -605,7 +610,7 @@
         vm(2, max(nbd, nx * nz), 8, LANES, dtype=F32),
         vm(2, 2, 2, ck, LANES),
         vm(2, 2, 2, ck, LANES),
-        dma((4,)),
+        dma((2, 2, 2)),
         dma((2, nbd - 1, 2)),
         dma((2, ny)),
         dma((2, ny - 1)),

time: 92 us -> 87.7 us (0.953)
  Pallas kernels: 89 us -> 84.7 us
    pallas_call x1, Pallas kernels: 89 us -> 84.7 us  [local(): pl.pallas_call(functools.partial(kernel, (cols, sizes)), out_shape=jax.Sh...]
where the time goes in v7:
time: 87.7 us; the launch traced here: 87.6 us
  Pallas kernels  84.7 us (97%)
  local copies, waits for them, and re-layouts  2.24 us (3%)
    pallas_call x1, Pallas kernels, local(): pl.pallas_call(functools.partial(kernel, (cols, sizes)), out_shape=jax.Sh...  84.7 us
    squeeze x1, local copies, waits for them, and re-layouts, local(): return (both[0, :, :, :cols], both[1, :, :, :cols])  2.24 us

profile of v7, /device:TPU:1, one launch (start us, length us, event | category | flops | bytes accessed | tf_op | source)
XLA Modules:
  0.0 87.6 jit_solution(7281405381202851595)
XLA Ops:
  0.6 84.7 %shard_map.68 = f32[2,32,32,128]{3,2,1,0:T(8,128)} custom-call(bf16[28,32,680]{2,1,0:T(8,128)(2,1)} %obs.1, f32[28,25]{1,0:T(8,128)} %row_taps.1, f32[28,25]{1,0:T(8,128)} %col_taps.1, bf16[32,224]{1,0:T(8,128)(2,1)} %bitcast.6, f32[1,32]{1,0:T(1,128)} %bitcast.7), custom_call_target="tpu_custom_call" | custom-call | tf_op jit(solution)/shard_map/pallas_call | solution.py:622
  85.3 2.2 %slice_bitcast_fusion = (f32[32,32,85]{2,1,0:T(8,128)}, f32[32,32,85]{2,1,0:T(8,128)}) fusion(f32[2,32,32,128]{3,2,1,0:T(8,128)} %shard_map.68), kind=kLoop, calls=%fused_computation | loop fusion | bytes 1392640 | tf_op jit(solution)/shard_map/squeeze | solution.py:632

commit v8 on v7

--- a/solution.py
+++ b/solution.py
@@ -302,7 +302,7 @@
             lax.fori_loop(third * q // 8, min(third * (q + 1), bands) // 8, place, 0)
         return carry
 
-    lax.fori_loop(0, rows // 16, rr_pair, 0)
+    lax.fori_loop(0, ku // 48, functools.partial(tt_pair, depth=SLOT), 0)
 
     above_ok, below_ok = i_row > 0, i_row < nrow - 1
 
@@ -373,7 +373,7 @@
         if idx:
             merge(idx - 1)
     merge(len(offsets) - 1)
-    lax.fori_loop(0, ku // 16, functools.partial(tt_pair, depth=SLOT), 0)
+    lax.fori_loop(ku // 48, ku // 16, functools.partial(tt_pair, depth=SLOT), 0)
 
     @pl.when(first | last)
     def _():
@@ -451,13 +451,8 @@
                 spec[step * m : step * (m + 1), row : row + 16, :] = v
 
         def columns(lo, count):
-            def body(g, c):
-                for q in range(56):
-                    b = 56 * g + q
-                    mid[b, lo : lo + count] = mm(spec[b, lo : lo + count][:, :ku], tt[b]).astype(BF)
-                return c
-
-            lax.fori_loop(0, bands // 56, body, 0)
+            for b in range(bands):
+                mid[b, lo : lo + count] = mm(spec[b, lo : lo + count][:, :ku], tt[b]).astype(BF)
 
         packing(0, range(nblk))
         own_edges = [to((0, 0), (1, 0), 0, left), to((1, 0), (0, 0), 1, right)]
@@ -476,6 +471,11 @@
         for i in range(nblk // 2):
             expand(16 * i, block(2 * i, 0, 2 * i), block(2 * i + 1, 0, 2 * i + 1))
         columns(0, rows)
+
+        @pl.when(n == 0)
+        def _():
+            lax.fori_loop(0, rows // 16, rr_pair, 0)
+
         r_up.wait()
         r_down.wait()
         for k in range(2):
@@ -495,16 +495,11 @@
             )
         columns(rows, ext_r - rows)
 
-        def along(g, c):
-            for q in range(40):
-                t = 40 * g + q
-                v = jnp.concatenate([mid[t], mid[third + t], mid[2 * third + t]], axis=0)
-                v = mm(rr[t][:, : 3 * ext_r], v)
-                for k in range(3):
-                    fin[third * k + t] = v[rows * k : rows * (k + 1)]
-            return c
-
-        lax.fori_loop(0, third // 40, along, 0)
+        for t in range(third):
+            v = jnp.concatenate([mid[t], mid[third + t], mid[2 * third + t]], axis=0)
+            v = mm(rr[t][:, : 3 * ext_r], v)
+            for k in range(3):
+                fin[third * k + t] = v[rows * k : rows * (k + 1)]
 
         for i in range(nblk):
             v = fin[:bands, 8 * i : 8 * (i + 1), :].reshape(bands * 8, LANES).astype(BF)

time: 87.7 us -> 86.2 us (0.983)
  Pallas kernels: 84.7 us -> 83.2 us
    pallas_call x1, Pallas kernels: 84.7 us -> 83.2 us  [local(): pl.pallas_call(functools.partial(kernel, (cols, sizes)), out_shape=jax.Sh...]
where the time goes in v8:
time: 86.2 us; the launch traced here: 86.1 us
  Pallas kernels  83.2 us (97%)
  local copies, waits for them, and re-layouts  2.24 us (3%)
    pallas_call x1, Pallas kernels, local(): pl.pallas_call(functools.partial(kernel, (cols, sizes)), out_shape=jax.Sh...  83.2 us
    squeeze x1, local copies, waits for them, and re-layouts, local(): return (both[0, :, :, :cols], both[1, :, :, :cols])  2.24 us

profile of v8, /device:TPU:1, one launch (start us, length us, event | category | flops | bytes accessed | tf_op | source)
XLA Modules:
  0.0 86.1 jit_solution(5044977230567970313)
XLA Ops:
  0.6 83.2 %shard_map.68 = f32[2,32,32,128]{3,2,1,0:T(8,128)} custom-call(bf16[28,32,680]{2,1,0:T(8,128)(2,1)} %obs.1, f32[28,25]{1,0:T(8,128)} %row_taps.1, f32[28,25]{1,0:T(8,128)} %col_taps.1, bf16[32,224]{1,0:T(8,128)(2,1)} %bitcast.6, f32[1,32]{1,0:T(1,128)} %bitcast.7), custom_call_target="tpu_custom_call" | custom-call | tf_op jit(solution)/shard_map/pallas_call | solution.py:617
  83.9 2.2 %slice_bitcast_fusion = (f32[32,32,85]{2,1,0:T(8,128)}, f32[32,32,85]{2,1,0:T(8,128)}) fusion(f32[2,32,32,128]{3,2,1,0:T(8,128)} %shard_map.68), kind=kLoop, calls=%fused_computation | loop fusion | bytes 1392640 | tf_op jit(solution)/shard_map/squeeze | solution.py:627

commit v9 on v8

--- a/solution.py
+++ b/solution.py
@@ -47,9 +47,9 @@
 
 
 def kernel(
-    dims, obs, row_taps, col_taps, basis_t, ridge_in,
+    dims, obs_in, row_taps, col_taps, basis_t, ridge_in,
     out,
-    edges, feats, taps, ridge, raw, vpad, edge_in, line_in, lines, rows_adj, cols_adj, zed, keep, out_a, in_a, out_b, in_b,
+    obs, obs_sem, edges, feats, taps, ridge, raw, vpad, edge_in, line_in, lines, rows_adj, cols_adj, zed, keep, out_a, in_a, out_b, in_b,
     tt, rr, e8, p8, p8_own, spec, mid, fin, work, ext, pack, pack_in, vec, red_src, red_in, tight, tight_in,
     edge_sem, line_sem, a_sem, b_sem, row_sem, col_sem, red_sem,
 ):
@@ -93,6 +93,10 @@
     everyone = peers + peers_r + list(corners.values())
     for d in everyone:
         pl.semaphore_signal(barrier, inc=1, device_id=d, device_id_type=pl.DeviceIdType.MESH)
+
+    fetch = pltpu.make_async_copy(obs_in, obs, obs_sem)
+    fetch.start()
+    fetch.wait()
 
     def pack_edges(g, carry):
         sl = pl.ds(pl.multiple_of(4 * RAD * g, 16), 4 * RAD)
@@ -302,7 +306,8 @@
             lax.fori_loop(third * q // 8, min(third * (q + 1), bands) // 8, place, 0)
         return carry
 
-    lax.fori_loop(0, ku // 48, functools.partial(tt_pair, depth=SLOT), 0)
+    slabs = ku // 16
+    lax.fori_loop(1, 3, functools.partial(tt_pair, depth=SLOT), 0)
 
     above_ok, below_ok = i_row > 0, i_row < nrow - 1
 
@@ -373,7 +378,7 @@
         if idx:
             merge(idx - 1)
     merge(len(offsets) - 1)
-    lax.fori_loop(ku // 48, ku // 16, functools.partial(tt_pair, depth=SLOT), 0)
+    lax.fori_loop(3, slabs - 1, functools.partial(tt_pair, depth=SLOT), 0)
 
     @pl.when(first | last)
     def _():
@@ -466,6 +471,11 @@
             to((1, 2), (0, 2), 4, corners[-1, 1]),
             to((0, 2), (1, 2), 5, corners[-1, -1]),
         ]
+
+        @pl.when(n == 0)
+        def _():
+            lax.fori_loop(0, 2, lambda p, c: tt_pair(p * (slabs - 1), c, depth=SLOT), 0)
+
         for c in own_edges:
             c.wait()
         for i in range(nblk // 2):
@@ -571,6 +581,8 @@
 
     dma = pltpu.SemaphoreType.DMA
     scratch = [
+        vm(own, rows, width),
+        dma,
         vm(2, own * RAD, width),
         vm(4, pad_own, 256),
         vm(own, 8, LANES, dtype=F32),
@@ -617,7 +629,7 @@
     both = pl.pallas_call(
         functools.partial(kernel, (cols, sizes)),
         out_shape=jax.ShapeDtypeStruct((2, comps, rows, LANES), F32),
-        in_specs=[vmem] * 5,
+        in_specs=[pl.BlockSpec(memory_space=pl.ANY)] + [vmem] * 4,
         out_specs=vmem,
         scratch_shapes=scratch,
         compiler_params=pltpu.CompilerParams(

time: 86.2 us -> 86 us (level)
  no operation moved by 1% of the time
where the time goes in v9:
time: 86 us; the launch traced here: 85.8 us
  Pallas kernels  82.9 us (96%)
  local copies, waits for them, and re-layouts  2.24 us (3%)
    pallas_call x1, Pallas kernels, local(): pl.pallas_call(functools.partial(kernel, (cols, sizes)), out_shape=jax.Sh...  82.9 us
    squeeze x1, local copies, waits for them, and re-layouts, local(): return (both[0, :, :, :cols], both[1, :, :, :cols])  2.24 us

profile of v9, /device:TPU:1, one launch (start us, length us, event | category | flops | bytes accessed | tf_op | source)
XLA Modules:
  0.0 85.8 jit_solution(2558558975248098867)
XLA Ops:
  0.6 82.9 %shard_map.68 = f32[2,32,32,128]{3,2,1,0:T(8,128)} custom-call(bf16[28,32,680]{2,1,0:T(8,128)(2,1)} %obs_in.1, f32[28,25]{1,0:T(8,128)} %row_taps.1, f32[28,25]{1,0:T(8,128)} %col_taps.1, bf16[32,224]{1,0:T(8,128)(2,1)} %bitcast.6, f32[1,32]{1,0:T(1,128)} %bitcast.7), custom_call_target="tpu_custom_call" | custom-call | tf_op jit(solution)/shard_map/pallas_call | solution.py:629
  83.6 2.2 %slice_bitcast_fusion = (f32[32,32,85]{2,1,0:T(8,128)}, f32[32,32,85]{2,1,0:T(8,128)}) fusion(f32[2,32,32,128]{3,2,1,0:T(8,128)} %shard_map.68), kind=kLoop, calls=%fused_computation | loop fusion | bytes 1392640 | tf_op jit(solution)/shard_map/squeeze | solution.py:639

commit v10 on v9

--- a/solution.py
+++ b/solution.py
@@ -115,14 +115,16 @@
             device_id=device, device_id_type=pl.DeviceIdType.MESH,
         )
 
-    early = (own // 4 + 1) // 2
-    edge_copies = []
-    for part, sl in enumerate((pl.ds(0, 4 * RAD * early), pl.ds(4 * RAD * early, RAD * own - 4 * RAD * early))):
+    slabs_own = own // 4
+    starts = [0, slabs_own // 2, slabs_own - 1, slabs_own]
+    edge_copies = {}
+    for part in range(3):
+        sl = pl.ds(4 * RAD * starts[part], 4 * RAD * (starts[part + 1] - starts[part]))
         a = remote(edges.at[0, sl], edge_in.at[1, sl], edge_sem.at[0, part, 0], edge_sem.at[1, part, 0], up)
         b = remote(edges.at[1, sl], edge_in.at[0, sl], edge_sem.at[0, part, 1], edge_sem.at[1, part, 1], down)
         a.start()
         b.start()
-        edge_copies.append((a, b))
+        edge_copies[starts[part]] = (a, b)
 
     pad_own = feats.shape[1]
     raw[...] = jnp.zeros_like(raw)
@@ -332,18 +334,20 @@
                 zed[k, 4 * g + q] = u[rows * k : rows * (k + 1)]
 
     for g in range(own // 4):
-        if g in (0, early):
-            for c in edge_copies[g // max(early, 1)]:
-                c.wait()
+        for c in edge_copies.get(g, ()):
+            c.wait()
         adjoint(g)
 
     lane_k = iota((ck, LANES), 1)
     cut = LANES - cols
-    offsets = [s for s in (2, 1, 3, 0) if s < ny]
-    a_copies, b_copies = [], []
+    way = jnp.where(core == 0, ny - 1, 1)
+    offsets = [2, ny - way, way, 0]
+    hops = [way, ny - way, way]
+    swap = [0, 2, 1, 3]
+    a_copies, b_copies = [], {}
 
     def merge(idx):
-        a_copies[idx].wait()
+        a_copies[swap[idx]].wait_recv()
         done = idx == len(offsets) - 1
 
         def add(i):
@@ -354,14 +358,22 @@
                 vec[0, i] = add(i)
         else:
             b = pltpu.roll(add(1), cols, 1)
-            out_b[idx, 0] = jnp.where(lane_k < cols, add(0), b).astype(BF)
-            out_b[idx, 1] = jnp.where(lane_k < cols - cut, b, pltpu.roll(add(2), cols - cut, 1)).astype(BF)
-            out_b[idx, 2] = add(3).astype(BF)
+            tiles = [
+                jnp.where(lane_k < cols, add(0), b),
+                jnp.where(lane_k < cols - cut, b, pltpu.roll(add(2), cols - cut, 1)),
+                add(3),
+            ]
+            if idx == 2:
+                b_copies[0].wait()
+            for t, v in enumerate(tiles):
+                if idx == 2:
+                    v = v + in_b[0, t].astype(F32)
+                out_b[idx, t] = v.astype(BF)
         if not done:
-            dest = (lax.rem(y + offsets[idx], ny), core, x, z)
+            dest = (lax.rem(y + hops[idx], ny), core, x, z)
             c = remote(out_b.at[idx], in_b.at[idx], b_sem.at[0, idx], b_sem.at[1, idx], dest)
             c.start()
-            b_copies.append(c)
+            b_copies[idx] = c
 
     for idx, off in enumerate(offsets):
         k = lax.rem(y + off, ny)
@@ -372,13 +384,15 @@
             lo, hi = v[:, :LANES], v[:, LANES:]
             keep[idx, i] = jnp.where(core == 0, lo, hi)
             out_a[idx, i] = jnp.where(core == 0, hi, lo).astype(BF)
-        c = remote(out_a.at[idx], in_a.at[idx], a_sem.at[0, idx], a_sem.at[1, idx], partner)
+        c = remote(out_a.at[idx], in_a.at[swap[idx]], a_sem.at[0, idx], a_sem.at[1, swap[idx]], partner)
         c.start()
         a_copies.append(c)
-        if idx:
+        if idx in (1, 2):
             merge(idx - 1)
-    merge(len(offsets) - 1)
-    lax.fori_loop(3, slabs - 1, functools.partial(tt_pair, depth=SLOT), 0)
+    merge(3)
+    lax.fori_loop(3, slabs - 3, functools.partial(tt_pair, depth=SLOT), 0)
+    merge(2)
+    lax.fori_loop(slabs - 3, slabs - 1, functools.partial(tt_pair, depth=SLOT), 0)
 
     @pl.when(first | last)
     def _():
@@ -386,9 +400,11 @@
         lax.fori_loop(p0, p0 + 2, functools.partial(tt_pair, depth=256), 0)
 
     mid[pl.ds(bands, mid.shape[0] - bands)] = jnp.zeros((mid.shape[0] - bands, ext_r, LANES), BF)
-    for c in b_copies:
-        c.wait()
-    a, b, c = (sum(in_b[idx, t].astype(F32) for idx in range(ny - 1)) for t in range(3))
+    b_copies[1].wait()
+    b_copies[2].wait()
+    for c in a_copies:
+        c.wait_send()
+    a, b, c = (in_b[1, t].astype(F32) + in_b[2, t].astype(F32) for t in range(3))
     b1 = jnp.where(lane_k < cut, pltpu.roll(a, cut, 1), pltpu.roll(b, cut, 1))
     for i, v in enumerate((a, b1, pltpu.roll(b, 2 * cut, 1), c)):
         vec[0, i] = vec[0, i] + jnp.where(lane_k < cols, v, 0.0)
@@ -617,7 +633,7 @@
         vm(2, max(nbd, nx * nz), 8, LANES, dtype=F32),
         vm(2, 2, 2, ck, LANES),
         vm(2, 2, 2, ck, LANES),
-        dma((2, 2, 2)),
+        dma((2, 3, 2)),
         dma((2, nbd - 1, 2)),
         dma((2, ny)),
         dma((2, ny - 1)),

time: 86 us -> 84.8 us (0.986)
  Pallas kernels: 82.9 us -> 81.8 us
    pallas_call x1, Pallas kernels: 82.9 us -> 81.8 us  [local(): pl.pallas_call(functools.partial(kernel, (cols, sizes)), out_shape=jax.Sh...]
where the time goes in v10:
time: 84.8 us; the launch traced here: 84.6 us
  Pallas kernels  81.8 us (96%)
  local copies, waits for them, and re-layouts  2.24 us (3%)
    pallas_call x1, Pallas kernels, local(): pl.pallas_call(functools.partial(kernel, (cols, sizes)), out_shape=jax.Sh...  81.8 us
    squeeze x1, local copies, waits for them, and re-layouts, local(): return (both[0, :, :, :cols], both[1, :, :, :cols])  2.24 us

profile of v10, /device:TPU:1, one launch (start us, length us, event | category | flops | bytes accessed | tf_op | source)
XLA Modules:
  0.0 84.6 jit_solution(1264599209123932425)
XLA Ops:
  0.6 81.8 %shard_map.68 = f32[2,32,32,128]{3,2,1,0:T(8,128)} custom-call(bf16[28,32,680]{2,1,0:T(8,128)(2,1)} %obs_in.1, f32[28,25]{1,0:T(8,128)} %row_taps.1, f32[28,25]{1,0:T(8,128)} %col_taps.1, bf16[32,224]{1,0:T(8,128)(2,1)} %bitcast.6, f32[1,32]{1,0:T(1,128)} %bitcast.7), custom_call_target="tpu_custom_call" | custom-call | tf_op jit(solution)/shard_map/pallas_call | solution.py:645
  82.4 2.2 %slice_bitcast_fusion = (f32[32,32,85]{2,1,0:T(8,128)}, f32[32,32,85]{2,1,0:T(8,128)}) fusion(f32[2,32,32,128]{3,2,1,0:T(8,128)} %shard_map.68), kind=kLoop, calls=%fused_computation | loop fusion | bytes 1392640 | tf_op jit(solution)/shard_map/squeeze | solution.py:655
